TPU v7x, 32 devices: a 4x4x1 block of a 4x4x8 slice. The times are simulated.
32 devices in a mesh: dp: 1 (over z), ing: 4 (over y), grp: 8 (over x, core).
Axes of the slice: x: 4, y: 4, z: 1, core: 2. Of those that a mesh axis runs over, the one named last changes fastest.
The devices are a block of a 4x4x8 slice.
Arguments:
- tokens: bfloat16 [32768, 2048], P(('dp', 'grp', 'ing'))
- expert_ids: int32 [32768, 8], P(('dp', 'grp', 'ing'))
- gate_weights: float32 [32768, 8], P(('dp', 'grp', 'ing'))
- w_gate: bfloat16 [64, 2048, 1024], P(('grp', 'ing'))
- w_up: bfloat16 [64, 2048, 1024], P(('grp', 'ing'))
- w_down: bfloat16 [64, 1024, 2048], P(('grp', 'ing'))
Outputs:
- output: bfloat16 [32768, 2048], P(('dp', 'grp', 'ing'))
All inputs are finite; a program needn't handle non-finite values.
Results may differ from a plain program's by a relative error of at most 0.00163.
Values are sent between devices in bfloat16 or wider.
A program may use at most 768 MiB of HBM per device.

v0:
```python
import jax
import jax.numpy as jnp
from jax import lax
from jax.sharding import PartitionSpec as P


def cap_sizes(tokens_dev, top_k, groups, group_exp):
    group_limit = min(groups // 2, top_k // 2)
    per_group = top_k // group_limit
    group_cap = 3 * tokens_dev * group_limit // (2 * groups)
    expert_cap = (group_cap * per_group + group_exp - 1) // group_exp
    return group_cap, expert_cap


def expert_ffn(expert_rows, gate_w, up_w, down_w):
    act_gate = jnp.einsum('lrd,ldf->lrf', expert_rows, gate_w, preferred_element_type=jnp.float32)
    act_up = jnp.einsum('lrd,ldf->lrf', expert_rows, up_w, preferred_element_type=jnp.float32)
    hidden = (jax.nn.silu(act_gate) * act_up).astype(jnp.bfloat16)
    return jnp.einsum('lrf,lfd->lrd', hidden, down_w, preferred_element_type=jnp.float32).astype(jnp.bfloat16)


def send_slots(ids_src, groups, group_exp, group_cap):
    tokens_dev = ids_src.shape[0]
    member = jnp.any(ids_src[:, :, None] // group_exp == jnp.arange(groups), axis=1)
    member_int = member.astype(jnp.int32)
    rank_pos = jnp.where(member, jnp.cumsum(member_int, axis=0) - member_int, group_cap)
    token_idx = jnp.broadcast_to(jnp.arange(tokens_dev, dtype=jnp.int32)[:, None], rank_pos.shape)
    slot_tok = jnp.full((groups, group_cap), tokens_dev, jnp.int32)
    return slot_tok.at[jnp.arange(groups)[None, :], rank_pos].set(token_idx, mode='drop')


def fanout_table(ids_all, gates_all, group_id, group_exp, group_cap, expert_cap):
    groups = ids_all.shape[0]
    hit_mask = (ids_all - group_id * group_exp)[..., None] == jnp.arange(group_exp)
    chosen = jnp.any(hit_mask, axis=2)
    gate_sum = jnp.sum(jnp.where(hit_mask, gates_all[..., None], 0.0), axis=2)
    in_group = jnp.any(chosen, axis=2).astype(jnp.int32)
    src_row = jnp.arange(groups)[:, None] * group_cap + jnp.cumsum(in_group, axis=1) - in_group
    chosen_int = chosen.astype(jnp.int32)
    exp_slot = jnp.cumsum(chosen_int, axis=1) - chosen_int
    total_slots = group_exp * groups * expert_cap
    flat_pos = (jnp.arange(group_exp)[None, None, :] * groups + jnp.arange(groups)[:, None, None]) * expert_cap + exp_slot
    flat_pos = jnp.where(chosen, flat_pos, total_slots)
    slot_table = jnp.full((total_slots,), groups * group_cap, jnp.int32)
    slot_table = slot_table.at[flat_pos].set(jnp.broadcast_to(src_row[:, :, None], flat_pos.shape).astype(jnp.int32), mode='drop')
    gate_table = jnp.zeros((total_slots,), jnp.float32).at[flat_pos].set(gate_sum, mode='drop')
    return slot_table, gate_table


def solution(mesh):
    groups = mesh.shape['grp']
    inner_size = mesh.shape['ing']
    row_spec = P(('dp', 'grp', 'ing'), None)
    weight_spec = P(('grp', 'ing'), None, None)

    def device_step(tokens, expert_ids, gate_weights, w_gate, w_up, w_down):
        tokens_dev, model_dim = tokens.shape
        top_k = expert_ids.shape[1]
        local_exp = w_gate.shape[0]
        group_exp = local_exp * inner_size
        group_cap, expert_cap = cap_sizes(tokens_dev, top_k, groups, group_exp)
        group_id = lax.axis_index('grp')
        slot_tok = send_slots(expert_ids, groups, group_exp, group_cap)
        send_rows = jnp.take(tokens, slot_tok.reshape(-1), axis=0, mode='fill', fill_value=0)
        send_rows = send_rows.reshape(groups, group_cap, model_dim)
        ids_all = lax.all_gather(expert_ids, 'grp')
        gates_all = lax.all_gather(gate_weights, 'grp')
        recv_rows = lax.all_to_all(send_rows, 'grp', 0, 0, tiled=True)
        slot_table, gate_table = fanout_table(ids_all, gates_all, group_id, group_exp, group_cap, expert_cap)
        fan_rows = jnp.take(recv_rows.reshape(groups * group_cap, model_dim), slot_table, axis=0, mode='fill', fill_value=0)
        fan_rows = fan_rows.reshape(inner_size, local_exp, groups * expert_cap, model_dim)
        expert_in = lax.all_to_all(fan_rows, 'ing', 0, 2, tiled=True)
        expert_in = expert_in.reshape(local_exp, inner_size * groups * expert_cap, model_dim)
        expert_out = expert_ffn(expert_in, w_gate, w_up, w_down)
        expert_out = expert_out.reshape(local_exp, inner_size, groups * expert_cap, model_dim)
        back_rows = lax.all_to_all(expert_out, 'ing', 1, 0, tiled=True).reshape(-1, model_dim)
        weighted = back_rows.astype(jnp.float32) * gate_table[:, None]
        group_sum = jax.ops.segment_sum(weighted, slot_table, num_segments=groups * group_cap)
        group_sum = group_sum.astype(jnp.bfloat16).reshape(groups, group_cap, model_dim)
        ret_rows = lax.all_to_all(group_sum, 'grp', 0, 0, tiled=True)
        combined = jax.ops.segment_sum(ret_rows.reshape(-1, model_dim).astype(jnp.float32), slot_tok.reshape(-1), num_segments=tokens_dev)
        return combined.astype(jnp.bfloat16)

    return jax.shard_map(device_step, mesh=mesh, in_specs=(row_spec, row_spec, row_spec, weight_spec, weight_spec, weight_spec), out_specs=row_spec, check_vma=False)
```

profile of v0, /device:TPU:97, one launch (start us, length us, event | category | flops | bytes accessed | tf_op | source)
XLA Modules:
  0.0 2877.8 jit_solution(13367298656937563489)
XLA Ops:
  5.9 30.5 %scatter_custom_fusion.4 = s32[6144]{0:T(1024)S(1)} fusion(s32[8192]{0:T(1024)S(1)} %reshape.263, s32[8192]{0:T(1024)S(1)} %reshape.265, s32[]{:T(128)} %constant.39.clone.1), kind=kCustom, calls=%fused_computation.69 | custom fusion | bytes 24580 | tf_op jit(solution)/shard_map/broadcast_in_dim;reshape | solution.py:81
  36.5 49.1 %gather_fusion = bf16[6144,2048]{1,0:T(8,128)(2,1)} fusion(bf16[1024,2048]{1,0:T(8,128)(2,1)} %param.6, s32[6144]{0:T(1024)S(1)} %broadcast_clamp_fusion), kind=kCustom, calls=%fused_computation | custom fusion | bytes 50356224 | tf_op jit(solution)/shard_map/jit(_take)/gather | solution.py:64
  85.6 21.0 broadcast_select_fusion.1
  106.5 8.4 all-to-all-start
  115.0 284.6 %all-gather = s32[8192,8]{0,1:T(8,128)S(1)} all-gather(s32[1024,8]{0,1:T(8,128)S(1)} %copy-done.5), channel_id=2, replica_groups=mesh['dp'=1,'ing'=4,'grp'=8] {'grp'}, dimensions={0}, use_global_device_ids=true | all-gather | bytes 294912 | tf_op jit(solution)/shard_map/all_gather | solution.py:66
  403.5 18.0 reduce-window.24
  424.4 2.7 copy.34
  427.0 3.6 reshape.233
  430.8 3.9 broadcast_in_dim.106
  434.8 3.6 reshape.235
  438.4 240.1 %scatter_custom_fusion = s32[12288]{0:T(1024)S(1)} fusion(s32[65536]{0:T(1024)S(1)} %reshape.233, s32[65536]{0:T(1024)S(1)} %reshape.235, s32[]{:T(128)} %constant.55.clone.1), kind=kCustom, calls=%fused_computation.64 | custom fusion | bytes 49156 | tf_op jit(solution)/shard_map/scatter | solution.py:45
  678.6 102.7 %gather_fusion.1 = bf16[12288,2048]{1,0:T(8,128)(2,1)} fusion(bf16[6144,2048]{1,0:T(8,128)(2,1)} %bitcast.12, s32[12288]{0:T(1024)S(1)} %fusion.13), kind=kCustom, calls=%fused_computation.1 | custom fusion | bytes 100712448 | tf_op jit(solution)/shard_map/jit(_take)/gather | solution.py:70
  781.3 33.6 %broadcast_select_fusion = bf16[4,2,1536,2048]{3,2,1,0:T(8,128)(2,1)} fusion(bf16[4,2,1536,2048]{3,2,1,0:T(8,128)(2,1)} %bitcast.74, pred[4,2,1536]{2,1,0:T(4,128)(4,1)S(1)} %broadcast_in_dim.108), kind=kLoop, calls=%fused_computation.12 | loop fusion | flops 25165824 | bytes 100675584 | tf_op jit(solution)/shard_map/jit(_take)/select_n | solution.py:70
  815.0 564.6 %all_to_all.34 = bf16[4,2,1536,2048]{3,2,1,0:T(8,128)(2,1)} all-to-all(bf16[4,2,1536,2048]{3,2,1,0:T(8,128)(2,1)} %broadcast_select_fusion), channel_id=1, replica_groups=mesh['dp'=1,'ing'=4,'grp'=8] {'ing'}, dimensions={0} | all-to-all | bytes 100663296 | tf_op jit(solution)/shard_map/all_to_all | solution.py:72
  1379.6 33.3 %copy.36 = bf16[1,2,4,1536,2048]{4,3,2,1,0:T(8,128)(2,1)} copy(bf16[1,2,4,1536,2048]{4,3,1,2,0:T(8,128)(2,1)} %bitcast.73) | data formatting | bytes 100663296 | tf_op jit(solution)/shard_map/all_to_all | solution.py:72
  1412.9 61.3 %fusion.25 = f32[2,6144,1024]{2,1,0:T(8,128)} fusion(bf16[2,6144,2048]{2,1,0:T(8,128)(2,1)} %bitcast.78, bf16[2,2048,1024]{2,1,0:T(8,128)(2,1)} %param.9), kind=kOutput, calls=%fused_computation.75 | convolution fusion | flops 51539607552 | bytes 109051904 | tf_op jit(solution)/shard_map/lrd,ldf->lrf/dot_general | solution.py:16
  1474.2 66.5 %multiply_convert_fusion.4 = bf16[2,6144,1024]{2,1,0:T(8,128)(2,1)} fusion(f32[2,6144,1024]{2,1,0:T(8,128)} %fusion.25, bf16[2,6144,2048]{2,1,0:T(8,128)(2,1)} %bitcast.79, bf16[2,2048,1024]{2,1,0:T(8,128)(2,1)} %param.10), kind=kOutput, calls=%fused_computation.11.clone.clone.1 | convolution fusion | flops 51615105024 | bytes 134217728 | tf_op jit(solution)/shard_map/lrd,ldf->lrf/dot_general | solution.py:17
  1540.8 61.9 %convolution_convert_fusion = bf16[2,6144,2048]{2,1,0:T(8,128)(2,1)} fusion(bf16[2,1024,2048]{2,1,0:T(8,128)(2,1)} %param.11, bf16[2,6144,1024]{2,1,0:T(8,128)(2,1)} %multiply_convert_fusion.4), kind=kOutput, calls=%fused_computation.13 | convolution fusion | flops 51564773376 | bytes 83886080 | tf_op jit(solution)/shard_map/lrf,lfd->lrd/dot_general | solution.py:19
  1602.7 33.3 %copy.37 = bf16[2,4,1536,2048]{3,2,0,1:T(8,128)(2,1)} copy(bf16[2,4,1536,2048]{3,2,1,0:T(8,128)(2,1)} %bitcast.80) | data formatting | bytes 100663296 | tf_op jit(solution)/shard_map/reshape | solution.py:75
  1636.0 12.1 all-to-all-start.2
  1648.1 23.3 all-gather.1
  1671.7 2.7 copy.38
  1674.3 3.6 reshape.243
  1678.0 240.0 %scatter_custom_fusion.1 = f32[12288]{0:T(1024)S(1)} fusion(s32[65536]{0:T(1024)} %copy-done.3, f32[65536]{0:T(1024)S(1)} %reshape.243, f32[]{:T(128)} %constant.32.clone.1), kind=kCustom, calls=%fused_computation.62 | custom fusion | bytes 49664 | tf_op jit(solution)/shard_map/scatter | solution.py:46
  1918.0 267.7 %all-to-all-done.2 = bf16[2,4,1536,2048]{3,2,0,1:T(8,128)(2,1)} async-done(((bf16[2,4,1536,2048]{3,2,0,1:T(8,128)(2,1)}), bf16[2,4,1536,2048]{3,2,0,1:T(8,128)(2,1)}, u32[]{:S(2)}, u32[]{:S(2)}) %all-to-all-start.2) | async-done | bytes 50331680 | tf_op jit(solution)/shard_map/all_to_all | solution.py:76
  2185.7 49.8 %bitcast_convert_fusion = f32[2,4,1,1536,2048]{4,3,0,1,2:T(8,128)} fusion(bf16[2,4,1536,2048]{3,2,0,1:T(8,128)(2,1)} %all-to-all-done.2), kind=kLoop, calls=%fused_computation.10 | loop fusion | flops 25165824 | bytes 150994944 | tf_op jit(solution)/shard_map/convert_element_type | solution.py:77
  2235.5 66.4 %bitcast_multiply_fusion = f32[12288,2048]{1,0:T(8,128)} fusion(f32[2,4,1,1536,2048]{4,3,0,1,2:T(8,128)} %bitcast_convert_fusion, f32[12288]{0:T(1024)S(1)} %scatter_custom_fusion.1), kind=kLoop, calls=%fused_computation.7 | loop fusion | flops 25165824 | bytes 201375744 | tf_op jit(solution)/shard_map/mul | solution.py:77
  2301.9 171.5 %scatter_custom_fusion.2 = f32[6144,2048]{1,0:T(8,128)} fusion(s32[12288]{0:T(1024)} %copy-done.2, f32[12288,2048]{1,0:T(8,128)} %bitcast_multiply_fusion, f32[]{:T(128)} %constant.32.clone.1), kind=kCustom, calls=%fused_computation.15 | custom fusion | flops 25165824 | bytes 50332160 | tf_op jit(solution)/shard_map/scatter-add | solution.py:78
  2473.5 25.9 convert_element_type.70
  2499.4 289.0 %all_to_all.35 = bf16[8,768,2048]{2,1,0:T(8,128)(2,1)} all-to-all(bf16[8,768,2048]{2,1,0:T(8,128)(2,1)} %bitcast.76), channel_id=1, replica_groups=mesh['dp'=1,'ing'=4,'grp'=8] {'grp'}, dimensions={0} | all-to-all | bytes 50331648 | tf_op jit(solution)/shard_map/all_to_all | solution.py:80
  2788.3 83.2 %scatter_custom_fusion.3 = f32[1024,2048]{1,0:T(8,128)} fusion(s32[6144]{0:T(1024)} %copy-done.4, bf16[6144,2048]{1,0:T(8,128)(2,1)} %bitcast.75, f32[]{:T(128)} %constant.32.clone.1), kind=kCustom, calls=%fused_computation.8 | custom fusion | flops 25165824 | bytes 33554944 | tf_op jit(solution)/shard_map/scatter-add | solution.py:81
  2871.5 6.0 convert_element_type.73
  (59 shorter events, 13.2 us)
Async XLA Ops:
  36.4 49.2 %copy-start.4 = (s32[6144]{0:T(1024)}, s32[6144]{0:T(1024)S(1)}, u32[]{:S(2)}) copy-start(s32[6144]{0:T(1024)S(1)} %scatter_custom_fusion.4) | copy-start | bytes 73732
  106.5 8.4 copy-start.5
  106.5 572.1 %all-to-all-start = ((bf16[8,768,2048]{2,1,0:T(8,128)(2,1)}), bf16[8,768,2048]{2,1,0:T(8,128)(2,1)}, u32[]{:S(2)}, u32[]{:S(2)}) async-start(bf16[8,768,2048]{2,1,0:T(8,128)(2,1)} %broadcast_select_fusion.1), calls=%async_computation | async-start | bytes 50331648 | tf_op jit(solution)/shard_map/all_to_all | solution.py:68
  399.6 0.7 copy-start
  430.7 350.7 %copy-start.3 = (s32[65536]{0:T(1024)}, s32[65536]{0:T(1024)S(1)}, u32[]{:S(2)}) copy-start(s32[65536]{0:T(1024)S(1)} %reshape.233) | copy-start | bytes 786436
  678.5 102.8 %copy-start.2 = (s32[12288]{0:T(1024)}, s32[12288]{0:T(1024)S(1)}, u32[]{:S(2)}) copy-start(s32[12288]{0:T(1024)S(1)} %scatter_custom_fusion) | copy-start | bytes 147460
  1636.0 12.1 copy-start.6
  1636.0 35.4 %copy-start.1 = (s32[8192,8]{0,1:T(8,128)S(1)}, s32[8192,8]{0,1:T(8,128)}, u32[]{:S(2)}) copy-start(s32[8192,8]{0,1:T(8,128)} %copy-done) | copy-start | bytes 786436
  1636.0 549.7 %all-to-all-start.2 = ((bf16[2,4,1536,2048]{3,2,0,1:T(8,128)(2,1)}), bf16[2,4,1536,2048]{3,2,0,1:T(8,128)(2,1)}, u32[]{:S(2)}, u32[]{:S(2)}) async-start(bf16[2,4,1536,2048]{3,2,0,1:T(8,128)(2,1)} %copy.37), calls=%async_computation.2 | async-start | bytes 100663296 | tf_op jit(solution)/shard_map/all_to_all | solution.py:76
where the time goes:
time: 2890 us; the launch traced here: 2880 us
  blocking collectives  1160 us (40%)
  local copies, waits for them, and re-layouts  753 us (26%)
  other arithmetic  485 us (17%)
  waiting for transfers between devices  268 us (9%)
  matrix products  190 us (7%)
    all_to_all x1, blocking collectives, device_step(): expert_in = lax.all_to_all(fan_rows, 'ing', 0, 2, tiled=True)  565 us
    all_to_all x1, blocking collectives, device_step(): ret_rows = lax.all_to_all(group_sum, 'grp', 0, 0, tiled=True)  289 us
    all_gather x1, blocking collectives, device_step(): ids_all = lax.all_gather(expert_ids, 'grp')  285 us
    all_to_all x1, waiting for transfers between devices, device_step(): lax.all_to_all(expert_out, 'ing', 1, 0, tiled=True).reshape(-1, model_dim)  268 us
    scatter x1, local copies, waits for them, and re-layouts, fanout_table(): slot_table.at[flat_pos]  240 us
    scatter x1, local copies, waits for them, and re-layouts, fanout_table(): jnp.zeros((total_slots,), jnp.float32).at[flat_pos]  240 us
    scatter-add x1, other arithmetic, device_step(): jax.ops.segment_sum(weighted, slot_table, num_segments=groups * group_cap)  172 us
    gather x1, local copies, waits for them, and re-layouts, device_step(): jnp.take(recv_rows.reshape(groups * group_cap, model_dim), slot_table, ax...  103 us
  transfers between devices with their start and end apart: 2, of which 1 were waited for; matrix products, arithmetic and copies ran while one was open for 18% of the time, Pallas kernels for 0%

commit v1 on v0

v1 whole, which is shorter than its diff:
```python
import functools

import jax
import jax.numpy as jnp
from jax import lax
from jax.experimental import pallas as pl
from jax.experimental.pallas import tpu as pltpu
from jax.sharding import PartitionSpec as P


LANES = 128


def cap_sizes(tokens_dev, top_k, groups, group_exp):
    group_limit = min(groups // 2, top_k // 2)
    per_group = top_k // group_limit
    group_cap = 3 * tokens_dev * group_limit // (2 * groups)
    expert_cap = (group_cap * per_group + group_exp - 1) // group_exp
    return per_group, expert_cap


def ffn_kernel(x_ref, gate_ref, up_ref, down_a_ref, down_b_ref, out_ref):
    rows = x_ref[...]
    act_gate = jnp.dot(rows, gate_ref[...], preferred_element_type=jnp.float32)
    act_up = jnp.dot(rows, up_ref[...], preferred_element_type=jnp.float32)
    hidden = (act_gate * jax.nn.sigmoid(act_gate) * act_up).astype(jnp.bfloat16)
    half = down_a_ref.shape[1]
    for part, down_ref in enumerate((down_a_ref, down_b_ref)):
        out = jnp.dot(hidden, down_ref[...], preferred_element_type=jnp.float32)
        out = out.astype(jnp.bfloat16).reshape(out.shape[0], half // LANES, LANES)
        out_ref[:, part * (half // LANES):(part + 1) * (half // LANES), :] = out


def expert_ffn(rows, gate_w, up_w, down_a, down_b, tile):
    count, dim = rows.shape
    ff = gate_w.shape[1]
    half = down_a.shape[1]
    fixed = lambda i: (0, 0)
    return pl.pallas_call(
        ffn_kernel,
        grid=(count // tile,),
        in_specs=[
            pl.BlockSpec((tile, dim), lambda i: (i, 0)),
            pl.BlockSpec((dim, ff), fixed),
            pl.BlockSpec((dim, ff), fixed),
            pl.BlockSpec((ff, half), fixed),
            pl.BlockSpec((ff, half), fixed),
        ],
        out_specs=pl.BlockSpec((tile, dim // LANES, LANES), lambda i: (i, 0, 0)),
        out_shape=jax.ShapeDtypeStruct((count, dim // LANES, LANES), jnp.bfloat16),
        compiler_params=pltpu.CompilerParams(vmem_limit_bytes=56 * 2**20),
        cost_estimate=pl.CostEstimate(flops=6 * count * dim * ff, bytes_accessed=4 * count * dim + 6 * dim * ff, transcendentals=count * ff),
    )(rows, gate_w, up_w, down_a, down_b)


def combine_kernel(per_group, top_k, pos_ref, gate_ref, *refs):
    sources, (out_ref, held, sems) = refs[:-3], refs[-3:]
    count = sources[0].shape[0]
    copies = [pltpu.make_async_copy(src, held.at[pl.ds(k * count, count)], sems.at[k]) for k, src in enumerate(sources)]
    for copy in copies:
        copy.start()
    for copy in copies:
        copy.wait()

    def one_token(tok, carry):
        total = None
        for first in range(0, top_k, per_group):
            partial = None
            for j in range(first, first + per_group):
                scaled = held[pos_ref[tok * top_k + j]].astype(jnp.float32) * gate_ref[tok * top_k + j]
                partial = scaled if partial is None else partial + scaled
            partial = partial.astype(jnp.bfloat16).astype(jnp.float32)
            total = partial if total is None else total + partial
        out_ref[tok] = total.astype(jnp.bfloat16)
        return carry

    lax.fori_loop(0, out_ref.shape[0], one_token, 0, unroll=4)


def combine(pos, gates, sources, per_group):
    tokens_dev, top_k = pos.shape
    count, subs, _ = sources[0].shape
    smem = pl.BlockSpec(memory_space=pltpu.SMEM)
    hbm = pl.BlockSpec(memory_space=pl.ANY)
    return pl.pallas_call(
        functools.partial(combine_kernel, per_group, top_k),
        in_specs=[smem, smem] + [hbm] * len(sources),
        out_specs=pl.BlockSpec(memory_space=pltpu.VMEM),
        out_shape=jax.ShapeDtypeStruct((tokens_dev, subs, LANES), jnp.bfloat16),
        scratch_shapes=[
            pltpu.VMEM((count * len(sources), subs, LANES), jnp.bfloat16),
            pltpu.SemaphoreType.DMA((len(sources),)),
        ],
        compiler_params=pltpu.CompilerParams(vmem_limit_bytes=60 * 2**20),
    )(pos.reshape(-1), gates.reshape(-1), *sources)


def solution(mesh):
    groups = mesh.shape['grp']
    inner_size = mesh.shape['ing']
    row_spec = P(('dp', 'grp', 'ing'), None)
    weight_spec = P(('grp', 'ing'), None, None)
    ahead = [(i, (i + 1) % inner_size) for i in range(inner_size)]
    behind = [(i, (i - 1) % inner_size) for i in range(inner_size)]

    def move(w, pairs):
        return lax.ppermute(w, 'ing', pairs)

    def device_step(tokens, expert_ids, gate_weights, w_gate, w_up, w_down):
        tokens_dev, dim = tokens.shape
        top_k = expert_ids.shape[1]
        local_exp = w_gate.shape[0]
        group_exp = local_exp * inner_size
        experts = group_exp * groups
        half = dim // 2
        per_group, expert_cap = cap_sizes(tokens_dev, top_k, groups, group_exp)
        inner = lax.axis_index('ing')

        own = [(w_gate[e], w_up[e], w_down[e][:, :half], w_down[e][:, half:]) for e in range(local_exp)]
        left = [tuple(move(w, ahead) for w in own[e]) for e in range(local_exp)]
        right = [tuple(move(w, behind) for w in own[e]) for e in range(local_exp)]
        far = [tuple(move((left, right)[k % 2][e][k], (ahead, behind)[k % 2]) for k in range(len(own[e]))) for e in range(local_exp)]

        shifts = (0, -1, 1, 2)
        held = {0: own, -1: left, 1: right, 2: far}
        phases = [(0, e) for e in range(local_exp)]
        phases += [(s, e) for e in range(local_exp) for s in (-1, 1)]
        phases += [(2, e) for e in range(local_exp)]
        assert inner_size == len(shifts)

        rows_all = lax.all_gather(tokens, 'grp', tiled=True)
        picked = jnp.any(expert_ids[:, :, None] == jnp.arange(experts), axis=1)
        before = jnp.tril(jnp.ones((tokens_dev, tokens_dev), jnp.bfloat16))
        upto = jnp.dot(before, picked.astype(jnp.bfloat16), preferred_element_type=jnp.float32).astype(jnp.int32)
        slot_tok = jnp.sum((upto.T[:, None, :] <= jnp.arange(expert_cap)[None, :, None]).astype(jnp.int32), axis=2)
        slot_tok = jnp.minimum(slot_tok, tokens_dev - 1).reshape(groups, group_exp * expert_cap)
        slot_in = lax.all_to_all(slot_tok, 'grp', 0, 0, tiled=True).reshape(groups, group_exp, expert_cap)
        slot_in = slot_in + (jnp.arange(groups, dtype=jnp.int32) * tokens_dev)[:, None, None]

        order = jnp.sum((expert_ids[:, None, :] < expert_ids[:, :, None]).astype(jnp.int32), axis=2)
        pick = order[:, :, None] == jnp.arange(top_k)
        ids = jnp.sum(jnp.where(pick, expert_ids[:, :, None], 0), axis=1)
        gates = jnp.sum(jnp.where(pick, gate_weights[:, :, None], 0.0), axis=1)
        rank = jnp.sum(jnp.where(ids[:, :, None] == jnp.arange(experts), upto[:, None, :], 0), axis=2) - 1
        member = ids % group_exp
        phase = jnp.zeros_like(ids)
        for p, (shift, e) in enumerate(phases):
            phase = jnp.where(member == (inner + shift) % inner_size * local_exp + e, p, phase)
        pos = (phase * groups + ids // group_exp) * expert_cap + rank

        returned = []
        for shift, e in phases:
            which = (inner + shift) % inner_size * local_exp + e
            index = lax.dynamic_index_in_dim(slot_in, which, 1, keepdims=False).reshape(-1)
            rows = rows_all.at[index].get(mode='promise_in_bounds')
            out = expert_ffn(rows, *held[shift][e], tile=256)
            out = out.reshape(groups, expert_cap, dim // LANES, LANES)
            back = lax.all_to_all(out, 'grp', 0, 0, tiled=True)
            returned.append(back.reshape(groups * expert_cap, dim // LANES, LANES))
        return combine(pos, gates, returned, per_group).reshape(tokens_dev, dim)


    return jax.shard_map(device_step, mesh=mesh, in_specs=(row_spec, row_spec, row_spec, weight_spec, weight_spec, weight_spec), out_specs=row_spec, check_vma=False)
```

time: 2890 us -> 1370 us (0.47)
  blocking collectives: 1160 us -> 0 us
  local copies, waits for them, and re-layouts: 753 us -> 208 us
  waiting for transfers between devices: 268 us -> 783 us
  other arithmetic: 485 us -> 8.25 us
  Pallas kernels: 0 us -> 252 us
  matrix products: 190 us -> 0.58 us
  starting transfers between devices: 20.5 us -> 93 us
    all_to_all x2 -> x0, blocking collectives: 854 us -> none  [the longest x1 565 us: device_step(): expert_in = lax.all_to_all(fan_rows, 'ing', 0, 2, tiled=True)]
    ppermute x0 -> x24, waiting for transfers between devices: none -> 578 us  [move(): return lax.ppermute(w, 'ing', pairs)]
    scatter x3 -> x0, local copies, waits for them, and re-layouts: 480 us -> none  [the longest x1 240 us: fanout_table(): slot_table.at[flat_pos]]
    all_gather x2 -> x0, blocking collectives: 308 us -> none  [the longest x1 285 us: device_step(): ids_all = lax.all_gather(expert_ids, 'grp')]
    scatter-add x2 -> x0, other arithmetic: 255 us -> none  [the longest x1 172 us: device_step(): jax.ops.segment_sum(weighted, slot_table, num_segments=groups * group_cap)]
    pallas_call x0 -> x9, Pallas kernels: none -> 252 us  [the longest x8 220 us: expert_ffn(): pl.pallas_call(ffn_kernel, grid=(count // tile,), in_specs=[pl.BlockSpec(...]
    dot_general x3 -> x1, matrix products: 190 us -> 0.58 us  [device_step(): jnp.dot(before, picked.astype(jnp.bfloat16), preferred_element_type=jnp.f...]
    all_to_all x2 -> x9, waiting for transfers between devices: 268 us -> 83.1 us  [the longest x8 83.1 us: device_step(): back = lax.all_to_all(out, 'grp', 0, 0, tiled=True)]
  transfers between devices with their start and end apart: 2 -> 34, of which waited for: 1 -> 15; matrix products, arithmetic and copies ran while one was open for 18% -> 14% of each run, Pallas kernels for 0% -> 14%
where the time goes in v1:
time: 1370 us; the launch traced here: 1360 us
  waiting for transfers between devices  783 us (57%)
  Pallas kernels  252 us (18%)
  local copies, waits for them, and re-layouts  208 us (15%)
  starting transfers between devices  93 us (7%)
  between operations  14.3 us (1%)
    ppermute x24, waiting for transfers between devices, move(): return lax.ppermute(w, 'ing', pairs)  578 us
    pallas_call x8, Pallas kernels, expert_ffn(): pl.pallas_call(ffn_kernel, grid=(count // tile,), in_specs=[pl.BlockSpec(...  220 us
    gather x8, local copies, waits for them, and re-layouts, device_step(): rows = rows_all.at[index].get(mode='promise_in_bounds')  170 us
    all_gather x1, waiting for transfers between devices, device_step(): rows_all = lax.all_gather(tokens, 'grp', tiled=True)  121 us
    all_to_all x8, waiting for transfers between devices, device_step(): back = lax.all_to_all(out, 'grp', 0, 0, tiled=True)  83.1 us
    all_to_all x8, starting transfers between devices, device_step(): back = lax.all_to_all(out, 'grp', 0, 0, tiled=True)  61.4 us
    pallas_call x1, Pallas kernels, combine(): pl.pallas_call(functools.partial(combine_kernel, per_group, top_k), in_sp...  32.7 us
  transfers between devices with their start and end apart: 34, of which 15 were waited for; matrix products, arithmetic and copies ran while one was open for 14% of the time, Pallas kernels for 14%

profile of v1, /device:TPU:97, one launch (start us, length us, event | category | flops | bytes accessed | tf_op | source)
XLA Modules:
  0.0 1359.2 jit_solution(6856532351890273153)
XLA Ops:
  45.6 121.1 %all-gather.2.cloned.1.call-done = bf16[8192,2048]{1,0:T(8,128)(2,1)} async-done(((bf16[1024,2048]{1,0:T(8,128)(2,1)}), bf16[8192,2048]{1,0:T(8,128)(2,1)}) %all-gather.2.cloned.1.call-update) | async-done | bytes 33554448 | tf_op jit(solution)/shard_map/all_gather | solution.py:131
  166.7 21.2 %gather_fusion = bf16[1536,2048]{1,0:T(8,128)(2,1)} fusion(bf16[8192,2048]{1,0:T(8,128)(2,1)} %all-gather.2.cloned.1.call-done, s32[2048]{0:T(1024)S(1)} %pad_clamp_fusion.7), kind=kCustom, calls=%fused_computation | custom fusion | bytes 12589056 | tf_op jit(solution)/shard_map/gather | solution.py:155
  187.9 27.4 %shard_map.64 = bf16[1536,16,128]{2,1,0:T(8,128)(2,1)} custom-call(bf16[1536,2048]{1,0:T(8,128)(2,1)} %gather_fusion, bf16[2048,1024]{1,0:T(8,128)(2,1)} %get-tuple-element.23.gate_ref, bf16[2048,1024]{1,0:T(8,128)(2,1)} %get-tuple-element.16.up_ref, bf16[1024,1024]{1,0:T(8,128)(2,1)} %get-tuple-element.22.down_a_ref, ...), custom_call_target="tpu_custom_call" | custom-call | flops 19327352832 | bytes 25165824 | tf_op jit(solution)/shard_map/pallas_call | solution.py:39
  227.8 21.1 %gather_fusion.1 = bf16[1536,2048]{1,0:T(8,128)(2,1)} fusion(bf16[8192,2048]{1,0:T(8,128)(2,1)} %all-gather.2.cloned.1.call-done, s32[2048]{0:T(1024)S(1)} %pad_clamp_fusion.6), kind=kCustom, calls=%fused_computation.1 | custom fusion | bytes 12589056 | tf_op jit(solution)/shard_map/gather | solution.py:155
  248.9 27.5 %shard_map.65 = bf16[1536,16,128]{2,1,0:T(8,128)(2,1)} custom-call(bf16[1536,2048]{1,0:T(8,128)(2,1)} %gather_fusion.1, bf16[2048,1024]{1,0:T(8,128)(2,1)} %get-tuple-element.24.gate_ref, bf16[2048,1024]{1,0:T(8,128)(2,1)} %get-tuple-element.15.up_ref, bf16[1024,1024]{1,0:T(8,128)(2,1)} %get-tuple-element.20.down_a_ref, ...), custom_call_target="tpu_custom_call" | custom-call | flops 19327352832 | bytes 25165824 | tf_op jit(solution)/shard_map/pallas_call | solution.py:39
  276.4 14.9 %all-to-all-done.1 = bf16[8,192,16,128]{3,2,1,0:T(8,128)(2,1)} async-done(((bf16[8,192,16,128]{3,2,1,0:T(8,128)(2,1)}), bf16[8,192,16,128]{3,2,1,0:T(8,128)(2,1)}, u32[]{:S(2)}, u32[]{:S(2)}) %all-to-all-start.1) | async-done | bytes 6291488 | tf_op jit(solution)/shard_map/all_to_all | solution.py:158
  301.2 21.3 %gather_fusion.2 = bf16[1536,2048]{1,0:T(8,128)(2,1)} fusion(bf16[8192,2048]{1,0:T(8,128)(2,1)} %all-gather.2.cloned.1.call-done, s32[2048]{0:T(1024)S(1)} %pad_clamp_fusion.5), kind=kCustom, calls=%fused_computation.2 | custom fusion | bytes 12589056 | tf_op jit(solution)/shard_map/gather | solution.py:155
  322.5 126.1 %collective-permute-done.2.down_a_ref = bf16[1024,1024]{1,0:T(8,128)(2,1)} collective-permute-done((bf16[1024,1024]{1,0:T(8,128)(2,1)}, bf16[1024,1024]{1,0:T(8,128)(2,1)}, u32[]{:S(2)}, u32[]{:S(2)}) %collective-permute-start.2) | collective-permute-done | bytes 2097184 | tf_op jit(solution)/shard_map/ppermute | solution.py:107
  450.2 43.3 %collective-permute-done.3.down_b_ref = bf16[1024,1024]{1,0:T(8,128)(2,1)} collective-permute-done((bf16[1024,1024]{1,0:T(8,128)(2,1)S(1)}, bf16[1024,1024]{1,0:T(8,128)(2,1)}, u32[]{:S(2)}, u32[]{:S(2)}) %collective-permute-start.3) | collective-permute-done | bytes 2097184 | tf_op jit(solution)/shard_map/ppermute | solution.py:107
  493.5 27.5 %shard_map.66 = bf16[1536,16,128]{2,1,0:T(8,128)(2,1)} custom-call(bf16[1536,2048]{1,0:T(8,128)(2,1)} %gather_fusion.2, bf16[2048,1024]{1,0:T(8,128)(2,1)} %collective-permute-done.gate_ref, bf16[2048,1024]{1,0:T(8,128)(2,1)} %collective-permute-done.1.up_ref, bf16[1024,1024]{1,0:T(8,128)(2,1)} %collective-permute-done.2.down_a_ref, ...), custom_call_target="tpu_custom_call" | custom-call | flops 19327352832 | bytes 25165824 | tf_op jit(solution)/shard_map/pallas_call | solution.py:39
  529.5 21.3 %gather_fusion.3 = bf16[1536,2048]{1,0:T(8,128)(2,1)} fusion(bf16[8192,2048]{1,0:T(8,128)(2,1)} %all-gather.2.cloned.1.call-done, s32[2048]{0:T(1024)S(1)} %pad_clamp_fusion.4), kind=kCustom, calls=%fused_computation.3 | custom fusion | bytes 12589056 | tf_op jit(solution)/shard_map/gather | solution.py:155
  550.8 34.1 %collective-permute-done.6.down_a_ref = bf16[1024,1024]{1,0:T(8,128)(2,1)} collective-permute-done((bf16[1024,1024]{1,0:T(8,128)(2,1)}, bf16[1024,1024]{1,0:T(8,128)(2,1)}, u32[]{:S(2)}, u32[]{:S(2)}) %collective-permute-start.6) | collective-permute-done | bytes 2097184 | tf_op jit(solution)/shard_map/ppermute | solution.py:107
  585.1 44.6 %collective-permute-done.7.down_b_ref = bf16[1024,1024]{1,0:T(8,128)(2,1)} collective-permute-done((bf16[1024,1024]{1,0:T(8,128)(2,1)S(1)}, bf16[1024,1024]{1,0:T(8,128)(2,1)}, u32[]{:S(2)}, u32[]{:S(2)}) %collective-permute-start.7) | collective-permute-done | bytes 2097184 | tf_op jit(solution)/shard_map/ppermute | solution.py:107
  629.8 27.5 %shard_map.67 = bf16[1536,16,128]{2,1,0:T(8,128)(2,1)} custom-call(bf16[1536,2048]{1,0:T(8,128)(2,1)} %gather_fusion.3, bf16[2048,1024]{1,0:T(8,128)(2,1)} %collective-permute-done.4.gate_ref, bf16[2048,1024]{1,0:T(8,128)(2,1)} %collective-permute-done.5.up_ref, bf16[1024,1024]{1,0:T(8,128)(2,1)} %collective-permute-done.6.down_a_ref, ...), custom_call_target="tpu_custom_call" | custom-call | flops 19327352832 | bytes 25165824 | tf_op jit(solution)/shard_map/pallas_call | solution.py:39
  667.7 21.2 %gather_fusion.4 = bf16[1536,2048]{1,0:T(8,128)(2,1)} fusion(bf16[8192,2048]{1,0:T(8,128)(2,1)} %all-gather.2.cloned.1.call-done, s32[2048]{0:T(1024)S(1)} %pad_clamp_fusion.3), kind=kCustom, calls=%fused_computation.4 | custom fusion | bytes 12589056 | tf_op jit(solution)/shard_map/gather | solution.py:155
  688.9 67.2 %collective-permute-done.10.down_a_ref = bf16[1024,1024]{1,0:T(8,128)(2,1)} collective-permute-done((bf16[1024,1024]{1,0:T(8,128)(2,1)}, bf16[1024,1024]{1,0:T(8,128)(2,1)}, u32[]{:S(2)}, u32[]{:S(2)}) %collective-permute-start.10) | collective-permute-done | bytes 2097184 | tf_op jit(solution)/shard_map/ppermute | solution.py:107
  756.1 44.9 %collective-permute-done.11.down_b_ref = bf16[1024,1024]{1,0:T(8,128)(2,1)} collective-permute-done((bf16[1024,1024]{1,0:T(8,128)(2,1)S(1)}, bf16[1024,1024]{1,0:T(8,128)(2,1)}, u32[]{:S(2)}, u32[]{:S(2)}) %collective-permute-start.11) | collective-permute-done | bytes 2097184 | tf_op jit(solution)/shard_map/ppermute | solution.py:107
  801.0 27.5 %shard_map.68 = bf16[1536,16,128]{2,1,0:T(8,128)(2,1)} custom-call(bf16[1536,2048]{1,0:T(8,128)(2,1)} %gather_fusion.4, bf16[2048,1024]{1,0:T(8,128)(2,1)} %collective-permute-done.8.gate_ref, bf16[2048,1024]{1,0:T(8,128)(2,1)} %collective-permute-done.9.up_ref, bf16[1024,1024]{1,0:T(8,128)(2,1)} %collective-permute-done.10.down_a_ref, ...), custom_call_target="tpu_custom_call" | custom-call | flops 19327352832 | bytes 25165824 | tf_op jit(solution)/shard_map/pallas_call | solution.py:39
  836.7 21.3 %gather_fusion.5 = bf16[1536,2048]{1,0:T(8,128)(2,1)} fusion(bf16[8192,2048]{1,0:T(8,128)(2,1)} %all-gather.2.cloned.1.call-done, s32[2048]{0:T(1024)S(1)} %pad_clamp_fusion.2), kind=kCustom, calls=%fused_computation.5 | custom fusion | bytes 12589056 | tf_op jit(solution)/shard_map/gather | solution.py:155
  858.0 33.2 %collective-permute-done.14.down_a_ref = bf16[1024,1024]{1,0:T(8,128)(2,1)} collective-permute-done((bf16[1024,1024]{1,0:T(8,128)(2,1)}, bf16[1024,1024]{1,0:T(8,128)(2,1)}, u32[]{:S(2)}, u32[]{:S(2)}) %collective-permute-start.14) | collective-permute-done | bytes 2097184 | tf_op jit(solution)/shard_map/ppermute | solution.py:107
  894.6 41.4 %collective-permute-done.15.down_b_ref = bf16[1024,1024]{1,0:T(8,128)(2,1)} collective-permute-done((bf16[1024,1024]{1,0:T(8,128)(2,1)S(1)}, bf16[1024,1024]{1,0:T(8,128)(2,1)}, u32[]{:S(2)}, u32[]{:S(2)}) %collective-permute-start.15) | collective-permute-done | bytes 2097184 | tf_op jit(solution)/shard_map/ppermute | solution.py:107
  936.0 27.5 %shard_map.69 = bf16[1536,16,128]{2,1,0:T(8,128)(2,1)} custom-call(bf16[1536,2048]{1,0:T(8,128)(2,1)} %gather_fusion.5, bf16[2048,1024]{1,0:T(8,128)(2,1)} %collective-permute-done.12.gate_ref, bf16[2048,1024]{1,0:T(8,128)(2,1)} %collective-permute-done.13.up_ref, bf16[1024,1024]{1,0:T(8,128)(2,1)} %collective-permute-done.14.down_a_ref, ...), custom_call_target="tpu_custom_call" | custom-call | flops 19327352832 | bytes 25165824 | tf_op jit(solution)/shard_map/pallas_call | solution.py:39
  978.2 21.3 %gather_fusion.6 = bf16[1536,2048]{1,0:T(8,128)(2,1)} fusion(bf16[8192,2048]{1,0:T(8,128)(2,1)} %all-gather.2.cloned.1.call-done, s32[2048]{0:T(1024)S(1)} %pad_clamp_fusion.1), kind=kCustom, calls=%fused_computation.6 | custom fusion | bytes 12589056 | tf_op jit(solution)/shard_map/gather | solution.py:155
  999.5 24.1 %collective-permute-done.18.down_a_ref = bf16[1024,1024]{1,0:T(8,128)(2,1)S(1)} collective-permute-done((bf16[1024,1024]{1,0:T(8,128)(2,1)}, bf16[1024,1024]{1,0:T(8,128)(2,1)S(1)}, u32[]{:S(2)}, u32[]{:S(2)}) %collective-permute-start.18) | collective-permute-done | bytes 2097184 | tf_op jit(solution)/shard_map/ppermute | solution.py:107
  1023.6 47.3 %collective-permute-done.19.down_b_ref = bf16[1024,1024]{1,0:T(8,128)(2,1)} collective-permute-done((bf16[1024,1024]{1,0:T(8,128)(2,1)}, bf16[1024,1024]{1,0:T(8,128)(2,1)}, u32[]{:S(2)}, u32[]{:S(2)}) %collective-permute-start.19) | collective-permute-done | bytes 2097184 | tf_op jit(solution)/shard_map/ppermute | solution.py:107
  1071.0 27.5 %shard_map.70 = bf16[1536,16,128]{2,1,0:T(8,128)(2,1)} custom-call(bf16[1536,2048]{1,0:T(8,128)(2,1)} %gather_fusion.6, bf16[2048,1024]{1,0:T(8,128)(2,1)} %collective-permute-done.16.gate_ref, bf16[2048,1024]{1,0:T(8,128)(2,1)} %collective-permute-done.17.up_ref, bf16[1024,1024]{1,0:T(8,128)(2,1)} %copy-done.10, ...), custom_call_target="tpu_custom_call" | custom-call | flops 19327352832 | bytes 25165824 | tf_op jit(solution)/shard_map/pallas_call | solution.py:39
  1112.9 21.3 %gather_fusion.7 = bf16[1536,2048]{1,0:T(8,128)(2,1)} fusion(bf16[8192,2048]{1,0:T(8,128)(2,1)} %all-gather.2.cloned.1.call-done, s32[2048]{0:T(1024)S(1)} %pad_clamp_fusion), kind=kCustom, calls=%fused_computation.7 | custom fusion | bytes 12589056 | tf_op jit(solution)/shard_map/gather | solution.py:155
  1134.3 24.4 %collective-permute-done.22.down_a_ref = bf16[1024,1024]{1,0:T(8,128)(2,1)S(1)} collective-permute-done((bf16[1024,1024]{1,0:T(8,128)(2,1)}, bf16[1024,1024]{1,0:T(8,128)(2,1)S(1)}, u32[]{:S(2)}, u32[]{:S(2)}) %collective-permute-start.22) | collective-permute-done | bytes 2097184 | tf_op jit(solution)/shard_map/ppermute | solution.py:107
  1158.6 47.1 %collective-permute-done.23.down_b_ref = bf16[1024,1024]{1,0:T(8,128)(2,1)} collective-permute-done((bf16[1024,1024]{1,0:T(8,128)(2,1)}, bf16[1024,1024]{1,0:T(8,128)(2,1)}, u32[]{:S(2)}, u32[]{:S(2)}) %collective-permute-start.23) | collective-permute-done | bytes 2097184 | tf_op jit(solution)/shard_map/ppermute | solution.py:107
  1205.8 27.5 %shard_map.71 = bf16[1536,16,128]{2,1,0:T(8,128)(2,1)} custom-call(bf16[1536,2048]{1,0:T(8,128)(2,1)} %gather_fusion.7, bf16[2048,1024]{1,0:T(8,128)(2,1)} %collective-permute-done.20.gate_ref, bf16[2048,1024]{1,0:T(8,128)(2,1)} %collective-permute-done.21.up_ref, bf16[1024,1024]{1,0:T(8,128)(2,1)} %copy-done.11, ...), custom_call_target="tpu_custom_call" | custom-call | flops 19327352832 | bytes 25165824 | tf_op jit(solution)/shard_map/pallas_call | solution.py:39
  1244.6 68.2 %all-to-all-done.8 = bf16[8,192,16,128]{3,2,1,0:T(8,128)(2,1)} async-done(((bf16[8,192,16,128]{3,2,1,0:T(8,128)(2,1)}), bf16[8,192,16,128]{3,2,1,0:T(8,128)(2,1)}, u32[]{:S(2)}, u32[]{:S(2)}) %all-to-all-start.8) | async-done | bytes 6291488 | tf_op jit(solution)/shard_map/all_to_all | solution.py:158
  1312.9 32.7 %shard_map.72 = bf16[1024,16,128]{2,1,0:T(8,128)(2,1)} custom-call(s32[8192]{0:T(1024)} %fusion.11.pos_ref, f32[8192]{0:T(1024)} %reshape.346.gate_ref, bf16[1536,16,128]{2,1,0:T(8,128)(2,1)} %bitcast.5.refs_0_, bf16[1536,16,128]{2,1,0:T(8,128)(2,1)} %bitcast.10.refs_1_, bf16[1536,16,128]{2,1,0:T(8,128)(2,1)} %bitcast.12.refs_2_, ...), custom_call_target="tpu_custom_call" | custom-call | tf_op jit(solution)/shard_map/pallas_call | solution.py:85
  (129 shorter events, 140.5 us)
Async XLA Ops:
  6.5 160.1 %all-gather.2.cloned.1.call-start = ((), (), s32[]{:S(2)}) async-start(), calls=%async_computation.9 | async-start | bytes 37748736 | tf_op jit(solution)/shard_map/all_gather | solution.py:131
  215.3 76.0 %all-to-all-start.1 = ((bf16[8,192,16,128]{3,2,1,0:T(8,128)(2,1)}), bf16[8,192,16,128]{3,2,1,0:T(8,128)(2,1)}, u32[]{:S(2)}, u32[]{:S(2)}) async-start(bf16[8,192,16,128]{3,2,1,0:T(8,128)(2,1)} %bitcast.42), calls=%async_computation.1 | async-start | bytes 12582912 | tf_op jit(solution)/shard_map/all_to_all | solution.py:158
  220.1 273.4 %collective-permute-start = (bf16[2048,1024]{1,0:T(8,128)(2,1)}, bf16[2048,1024]{1,0:T(8,128)(2,1)}, u32[]{:S(2)}, u32[]{:S(2)}) collective-permute-start(bf16[2048,1024]{1,0:T(8,128)(2,1)} %get-tuple-element.23.gate_ref), channel_id=1, source_target_pairs={{0,8},{8,16},{16,24},{24,0},{1,9},{9,17},{17,25},{25,1},{2,10},{10... | collective-permute-start | bytes 12582920 | tf_op jit(solution)/shard_map/ppermute | solution.py:107
  221.6 271.9 %collective-permute-start.1 = (bf16[2048,1024]{1,0:T(8,128)(2,1)}, bf16[2048,1024]{1,0:T(8,128)(2,1)}, u32[]{:S(2)}, u32[]{:S(2)}) collective-permute-start(bf16[2048,1024]{1,0:T(8,128)(2,1)} %get-tuple-element.16.up_ref), channel_id=1, source_target_pairs={{0,8},{8,16},{16,24},{24,0},{1,9},{9,17},{17,25},{25,1},{2,10},{10... | collective-permute-start | bytes 12582920 | tf_op jit(solution)/shard_map/ppermute | solution.py:107
  291.3 229.7 %all-to-all-start.2 = ((bf16[8,192,16,128]{3,2,1,0:T(8,128)(2,1)}), bf16[8,192,16,128]{3,2,1,0:T(8,128)(2,1)}, u32[]{:S(2)}, u32[]{:S(2)}) async-start(bf16[8,192,16,128]{3,2,1,0:T(8,128)(2,1)} %bitcast.40), calls=%async_computation.2 | async-start | bytes 12582912 | tf_op jit(solution)/shard_map/all_to_all | solution.py:158
  297.1 151.5 %collective-permute-start.2 = (bf16[1024,1024]{1,0:T(8,128)(2,1)}, bf16[1024,1024]{1,0:T(8,128)(2,1)}, u32[]{:S(2)}, u32[]{:S(2)}) collective-permute-start(bf16[1024,1024]{1,0:T(8,128)(2,1)} %get-tuple-element.22.down_a_ref), channel_id=1, source_target_pairs={{0,8},{8,16},{16,24},{24,0},{1,9},{9,17},{17,25},{25,1},{2,10},{10... | collective-permute-start | bytes 6291464 | tf_op jit(solution)/shard_map/ppermute | solution.py:107
  298.4 195.1 %collective-permute-start.3 = (bf16[1024,1024]{1,0:T(8,128)(2,1)S(1)}, bf16[1024,1024]{1,0:T(8,128)(2,1)}, u32[]{:S(2)}, u32[]{:S(2)}) collective-permute-start(bf16[1024,1024]{1,0:T(8,128)(2,1)S(1)} %copy-done), channel_id=1, source_target_pairs={{0,8},{8,16},{16,24},{24,0},{1,9},{9,17},{17,25},{25,1},{2,10},{10... | collective-permute-start | bytes 6291464 | tf_op jit(solution)/shard_map/ppermute | solution.py:107
  299.8 330.0 %collective-permute-start.4 = (bf16[2048,1024]{1,0:T(8,128)(2,1)}, bf16[2048,1024]{1,0:T(8,128)(2,1)}, u32[]{:S(2)}, u32[]{:S(2)}) collective-permute-start(bf16[2048,1024]{1,0:T(8,128)(2,1)} %get-tuple-element.23.gate_ref), channel_id=1, source_target_pairs={{0,24},{8,0},{16,8},{24,16},{1,25},{9,1},{17,9},{25,17},{2,26},{10... | collective-permute-start | bytes 12582920 | tf_op jit(solution)/shard_map/ppermute | solution.py:107
  448.6 181.2 %collective-permute-start.5 = (bf16[2048,1024]{1,0:T(8,128)(2,1)}, bf16[2048,1024]{1,0:T(8,128)(2,1)}, u32[]{:S(2)}, u32[]{:S(2)}) collective-permute-start(bf16[2048,1024]{1,0:T(8,128)(2,1)} %get-tuple-element.16.up_ref), channel_id=1, source_target_pairs={{0,24},{8,0},{16,8},{24,16},{1,25},{9,1},{17,9},{25,17},{2,26},{10... | collective-permute-start | bytes 12582920 | tf_op jit(solution)/shard_map/ppermute | solution.py:107
  521.0 136.3 %all-to-all-start.3 = ((bf16[8,192,16,128]{3,2,1,0:T(8,128)(2,1)}), bf16[8,192,16,128]{3,2,1,0:T(8,128)(2,1)}, u32[]{:S(2)}, u32[]{:S(2)}) async-start(bf16[8,192,16,128]{3,2,1,0:T(8,128)(2,1)} %bitcast.36), calls=%async_computation.3 | async-start | bytes 12582912 | tf_op jit(solution)/shard_map/all_to_all | solution.py:158
  526.6 58.2 %collective-permute-start.6 = (bf16[1024,1024]{1,0:T(8,128)(2,1)}, bf16[1024,1024]{1,0:T(8,128)(2,1)}, u32[]{:S(2)}, u32[]{:S(2)}) collective-permute-start(bf16[1024,1024]{1,0:T(8,128)(2,1)} %get-tuple-element.22.down_a_ref), channel_id=1, source_target_pairs={{0,24},{8,0},{16,8},{24,16},{1,25},{9,1},{17,9},{25,17},{2,26},{10... | collective-permute-start | bytes 6291464 | tf_op jit(solution)/shard_map/ppermute | solution.py:107
  527.9 101.9 %collective-permute-start.7 = (bf16[1024,1024]{1,0:T(8,128)(2,1)S(1)}, bf16[1024,1024]{1,0:T(8,128)(2,1)}, u32[]{:S(2)}, u32[]{:S(2)}) collective-permute-start(bf16[1024,1024]{1,0:T(8,128)(2,1)S(1)} %copy-done), channel_id=1, source_target_pairs={{0,24},{8,0},{16,8},{24,16},{1,25},{9,1},{17,9},{25,17},{2,26},{10... | collective-permute-start | bytes 6291464 | tf_op jit(solution)/shard_map/ppermute | solution.py:107
  528.5 272.5 %collective-permute-start.8 = (bf16[2048,1024]{1,0:T(8,128)(2,1)}, bf16[2048,1024]{1,0:T(8,128)(2,1)}, u32[]{:S(2)}, u32[]{:S(2)}) collective-permute-start(bf16[2048,1024]{1,0:T(8,128)(2,1)} %get-tuple-element.24.gate_ref), channel_id=1, source_target_pairs={{0,8},{8,16},{16,24},{24,0},{1,9},{9,17},{17,25},{25,1},{2,10},{10... | collective-permute-start | bytes 12582920 | tf_op jit(solution)/shard_map/ppermute | solution.py:107
  584.8 216.2 %collective-permute-start.9 = (bf16[2048,1024]{1,0:T(8,128)(2,1)}, bf16[2048,1024]{1,0:T(8,128)(2,1)}, u32[]{:S(2)}, u32[]{:S(2)}) collective-permute-start(bf16[2048,1024]{1,0:T(8,128)(2,1)} %get-tuple-element.15.up_ref), channel_id=1, source_target_pairs={{0,8},{8,16},{16,24},{24,0},{1,9},{9,17},{17,25},{25,1},{2,10},{10... | collective-permute-start | bytes 12582920 | tf_op jit(solution)/shard_map/ppermute | solution.py:107
  657.3 171.2 %all-to-all-start.4 = ((bf16[8,192,16,128]{3,2,1,0:T(8,128)(2,1)}), bf16[8,192,16,128]{3,2,1,0:T(8,128)(2,1)}, u32[]{:S(2)}, u32[]{:S(2)}) async-start(bf16[8,192,16,128]{3,2,1,0:T(8,128)(2,1)} %bitcast.39), calls=%async_computation.4 | async-start | bytes 12582912 | tf_op jit(solution)/shard_map/all_to_all | solution.py:158
  664.5 91.5 %collective-permute-start.10 = (bf16[1024,1024]{1,0:T(8,128)(2,1)}, bf16[1024,1024]{1,0:T(8,128)(2,1)}, u32[]{:S(2)}, u32[]{:S(2)}) collective-permute-start(bf16[1024,1024]{1,0:T(8,128)(2,1)} %get-tuple-element.20.down_a_ref), channel_id=1, source_target_pairs={{0,8},{8,16},{16,24},{24,0},{1,9},{9,17},{17,25},{25,1},{2,10},{10... | collective-permute-start | bytes 6291464 | tf_op jit(solution)/shard_map/ppermute | solution.py:107
  664.8 136.2 %collective-permute-start.11 = (bf16[1024,1024]{1,0:T(8,128)(2,1)S(1)}, bf16[1024,1024]{1,0:T(8,128)(2,1)}, u32[]{:S(2)}, u32[]{:S(2)}) collective-permute-start(bf16[1024,1024]{1,0:T(8,128)(2,1)S(1)} %copy-done.1), channel_id=1, source_target_pairs={{0,8},{8,16},{16,24},{24,0},{1,9},{9,17},{17,25},{25,1},{2,10},{10... | collective-permute-start | bytes 6291464 | tf_op jit(solution)/shard_map/ppermute | solution.py:107
  665.6 270.4 %collective-permute-start.12 = (bf16[2048,1024]{1,0:T(8,128)(2,1)}, bf16[2048,1024]{1,0:T(8,128)(2,1)}, u32[]{:S(2)}, u32[]{:S(2)}) collective-permute-start(bf16[2048,1024]{1,0:T(8,128)(2,1)} %get-tuple-element.24.gate_ref), channel_id=1, source_target_pairs={{0,24},{8,0},{16,8},{24,16},{1,25},{9,1},{17,9},{25,17},{2,26},{10... | collective-permute-start | bytes 12582920 | tf_op jit(solution)/shard_map/ppermute | solution.py:107
  756.1 180.0 %collective-permute-start.13 = (bf16[2048,1024]{1,0:T(8,128)(2,1)}, bf16[2048,1024]{1,0:T(8,128)(2,1)}, u32[]{:S(2)}, u32[]{:S(2)}) collective-permute-start(bf16[2048,1024]{1,0:T(8,128)(2,1)} %get-tuple-element.15.up_ref), channel_id=1, source_target_pairs={{0,24},{8,0},{16,8},{24,16},{1,25},{9,1},{17,9},{25,17},{2,26},{10... | collective-permute-start | bytes 12582920 | tf_op jit(solution)/shard_map/ppermute | solution.py:107
  828.5 135.0 %all-to-all-start.5 = ((bf16[8,192,16,128]{3,2,1,0:T(8,128)(2,1)}), bf16[8,192,16,128]{3,2,1,0:T(8,128)(2,1)}, u32[]{:S(2)}, u32[]{:S(2)}) async-start(bf16[8,192,16,128]{3,2,1,0:T(8,128)(2,1)} %bitcast.37), calls=%async_computation.5 | async-start | bytes 12582912 | tf_op jit(solution)/shard_map/all_to_all | solution.py:158
  835.0 56.2 %collective-permute-start.14 = (bf16[1024,1024]{1,0:T(8,128)(2,1)}, bf16[1024,1024]{1,0:T(8,128)(2,1)}, u32[]{:S(2)}, u32[]{:S(2)}) collective-permute-start(bf16[1024,1024]{1,0:T(8,128)(2,1)} %get-tuple-element.20.down_a_ref), channel_id=1, source_target_pairs={{0,24},{8,0},{16,8},{24,16},{1,25},{9,1},{17,9},{25,17},{2,26},{10... | collective-permute-start | bytes 6291464 | tf_op jit(solution)/shard_map/ppermute | solution.py:107
  835.0 101.0 %collective-permute-start.15 = (bf16[1024,1024]{1,0:T(8,128)(2,1)S(1)}, bf16[1024,1024]{1,0:T(8,128)(2,1)}, u32[]{:S(2)}, u32[]{:S(2)}) collective-permute-start(bf16[1024,1024]{1,0:T(8,128)(2,1)S(1)} %copy-done.1), channel_id=1, source_target_pairs={{0,24},{8,0},{16,8},{24,16},{1,25},{9,1},{17,9},{25,17},{2,26},{10... | collective-permute-start | bytes 6291464 | tf_op jit(solution)/shard_map/ppermute | solution.py:107
  835.5 235.4 %collective-permute-start.16 = (bf16[2048,1024]{1,0:T(8,128)(2,1)}, bf16[2048,1024]{1,0:T(8,128)(2,1)}, u32[]{:S(2)}, u32[]{:S(2)}) collective-permute-start(bf16[2048,1024]{1,0:T(8,128)(2,1)} %collective-permute-done.gate_ref), channel_id=1, source_target_pairs={{0,8},{8,16},{16,24},{24,0},{1,9},{9,17},{17,25},{25,1},{2,10},{10... | collective-permute-start | bytes 12582920 | tf_op jit(solution)/shard_map/ppermute | solution.py:107
  891.2 179.8 %collective-permute-start.17 = (bf16[2048,1024]{1,0:T(8,128)(2,1)}, bf16[2048,1024]{1,0:T(8,128)(2,1)}, u32[]{:S(2)}, u32[]{:S(2)}) collective-permute-start(bf16[2048,1024]{1,0:T(8,128)(2,1)} %collective-permute-done.5.up_ref), channel_id=1, source_target_pairs={{0,24},{8,0},{16,8},{24,16},{1,25},{9,1},{17,9},{25,17},{2,26},{10... | collective-permute-start | bytes 12582920 | tf_op jit(solution)/shard_map/ppermute | solution.py:107
  963.5 134.9 %all-to-all-start.6 = ((bf16[8,192,16,128]{3,2,1,0:T(8,128)(2,1)}), bf16[8,192,16,128]{3,2,1,0:T(8,128)(2,1)}, u32[]{:S(2)}, u32[]{:S(2)}) async-start(bf16[8,192,16,128]{3,2,1,0:T(8,128)(2,1)} %bitcast.35), calls=%async_computation.6 | async-start | bytes 12582912 | tf_op jit(solution)/shard_map/all_to_all | solution.py:158
  975.3 95.7 %collective-permute-start.19 = (bf16[1024,1024]{1,0:T(8,128)(2,1)}, bf16[1024,1024]{1,0:T(8,128)(2,1)}, u32[]{:S(2)}, u32[]{:S(2)}) collective-permute-start(bf16[1024,1024]{1,0:T(8,128)(2,1)} %collective-permute-done.7.down_b_ref), channel_id=1, source_target_pairs={{0,24},{8,0},{16,8},{24,16},{1,25},{9,1},{17,9},{25,17},{2,26},{10... | collective-permute-start | bytes 6291464 | tf_op jit(solution)/shard_map/ppermute | solution.py:107
  978.1 227.7 %collective-permute-start.20 = (bf16[2048,1024]{1,0:T(8,128)(2,1)}, bf16[2048,1024]{1,0:T(8,128)(2,1)}, u32[]{:S(2)}, u32[]{:S(2)}) collective-permute-start(bf16[2048,1024]{1,0:T(8,128)(2,1)} %collective-permute-done.8.gate_ref), channel_id=1, source_target_pairs={{0,8},{8,16},{16,24},{24,0},{1,9},{9,17},{17,25},{25,1},{2,10},{10... | collective-permute-start | bytes 12582920 | tf_op jit(solution)/shard_map/ppermute | solution.py:107
  1023.6 182.2 %collective-permute-start.21 = (bf16[2048,1024]{1,0:T(8,128)(2,1)}, bf16[2048,1024]{1,0:T(8,128)(2,1)}, u32[]{:S(2)}, u32[]{:S(2)}) collective-permute-start(bf16[2048,1024]{1,0:T(8,128)(2,1)} %collective-permute-done.13.up_ref), channel_id=1, source_target_pairs={{0,24},{8,0},{16,8},{24,16},{1,25},{9,1},{17,9},{25,17},{2,26},{10... | collective-permute-start | bytes 12582920 | tf_op jit(solution)/shard_map/ppermute | solution.py:107
  1098.4 134.8 %all-to-all-start.7 = ((bf16[8,192,16,128]{3,2,1,0:T(8,128)(2,1)}), bf16[8,192,16,128]{3,2,1,0:T(8,128)(2,1)}, u32[]{:S(2)}, u32[]{:S(2)}) async-start(bf16[8,192,16,128]{3,2,1,0:T(8,128)(2,1)} %bitcast.38), calls=%async_computation.7 | async-start | bytes 12582912 | tf_op jit(solution)/shard_map/all_to_all | solution.py:158
  1109.9 48.8 %collective-permute-start.22 = (bf16[1024,1024]{1,0:T(8,128)(2,1)}, bf16[1024,1024]{1,0:T(8,128)(2,1)S(1)}, u32[]{:S(2)}, u32[]{:S(2)}) collective-permute-start(bf16[1024,1024]{1,0:T(8,128)(2,1)} %collective-permute-done.10.down_a_ref), channel_id=1, source_target_pairs={{0,8},{8,16},{16,24},{24,0},{1,9},{9,17},{17,25},{25,1},{2,10},{10... | collective-permute-start | bytes 6291464 | tf_op jit(solution)/shard_map/ppermute | solution.py:107
  1109.9 95.9 %collective-permute-start.23 = (bf16[1024,1024]{1,0:T(8,128)(2,1)}, bf16[1024,1024]{1,0:T(8,128)(2,1)}, u32[]{:S(2)}, u32[]{:S(2)}) collective-permute-start(bf16[1024,1024]{1,0:T(8,128)(2,1)} %collective-permute-done.15.down_b_ref), channel_id=1, source_target_pairs={{0,24},{8,0},{16,8},{24,16},{1,25},{9,1},{17,9},{25,17},{2,26},{10... | collective-permute-start | bytes 6291464 | tf_op jit(solution)/shard_map/ppermute | solution.py:107
  1233.3 79.6 %all-to-all-start.8 = ((bf16[8,192,16,128]{3,2,1,0:T(8,128)(2,1)}), bf16[8,192,16,128]{3,2,1,0:T(8,128)(2,1)}, u32[]{:S(2)}, u32[]{:S(2)}) async-start(bf16[8,192,16,128]{3,2,1,0:T(8,128)(2,1)} %bitcast.41), calls=%async_computation.8 | async-start | bytes 12582912 | tf_op jit(solution)/shard_map/all_to_all | solution.py:158
  (14 other events, 279.5 us)
Sparse Core Ops, SparseCore 0:
  9.0 157.6 all-gather.1

commit v2 on v1

v2 whole, which is shorter than its diff:
```python
import functools

import jax
import jax.numpy as jnp
from jax import lax
from jax.experimental import pallas as pl
from jax.experimental.pallas import tpu as pltpu
from jax.sharding import PartitionSpec as P


LANES = 128


def cap_sizes(tokens_dev, top_k, groups, group_exp):
    group_limit = min(groups // 2, top_k // 2)
    per_group = top_k // group_limit
    group_cap = 3 * tokens_dev * group_limit // (2 * groups)
    expert_cap = (group_cap * per_group + group_exp - 1) // group_exp
    return per_group, expert_cap


def gated_rows(x_ref, gate_ref, up_ref):
    rows = x_ref[...]
    act_gate = jnp.dot(rows, gate_ref[...], preferred_element_type=jnp.float32)
    act_up = jnp.dot(rows, up_ref[...], preferred_element_type=jnp.float32)
    return (act_gate * jax.nn.sigmoid(act_gate) * act_up).astype(jnp.bfloat16)


def down_rows(hidden, down_refs, out_ref):
    at = 0
    for down_ref in down_refs:
        subs = down_ref.shape[1] // LANES
        out = jnp.dot(hidden, down_ref[...], preferred_element_type=jnp.float32)
        out_ref[:, at:at + subs, :] = out.astype(jnp.bfloat16).reshape(out.shape[0], subs, LANES)
        at += subs


def ffn_kernel(x_ref, gate_ref, up_ref, *refs):
    down_rows(gated_rows(x_ref, gate_ref, up_ref), refs[:-1], refs[-1])


def hidden_kernel(x_ref, gate_ref, up_ref, out_ref):
    out_ref[...] = gated_rows(x_ref, gate_ref, up_ref)


def down_kernel(x_ref, *refs):
    down_rows(x_ref[...], refs[:-1], refs[-1])


def per_tile(kernel, rows, weights, out_tail, tile):
    count, dim = rows.shape
    weight_bytes = sum(2 * w.size for w in weights)
    out_size = count
    for n in out_tail:
        out_size *= n
    return pl.pallas_call(
        kernel,
        grid=(count // tile,),
        in_specs=[pl.BlockSpec((tile, dim), lambda i: (i, 0))] + [pl.BlockSpec(w.shape, lambda i: (0, 0)) for w in weights],
        out_specs=pl.BlockSpec((tile,) + out_tail, lambda i: (i,) + (0,) * len(out_tail)),
        out_shape=jax.ShapeDtypeStruct((count,) + out_tail, jnp.bfloat16),
        compiler_params=pltpu.CompilerParams(vmem_limit_bytes=56 * 2**20),
        cost_estimate=pl.CostEstimate(flops=count * weight_bytes, bytes_accessed=2 * rows.size + weight_bytes + 2 * out_size, transcendentals=0),
    )(rows, *weights)


def expert_ffn(rows, gate_w, up_w, downs, tile):
    return per_tile(ffn_kernel, rows, (gate_w, up_w) + downs, (sum(d.shape[1] for d in downs) // LANES, LANES), tile)


def expert_hidden(rows, gate_w, up_w, tile):
    return per_tile(hidden_kernel, rows, (gate_w, up_w), (gate_w.shape[1],), tile)


def expert_down(hidden, downs, tile):
    return per_tile(down_kernel, hidden, downs, (sum(d.shape[1] for d in downs) // LANES, LANES), tile)


def combine_kernel(per_group, top_k, part, pos_ref, gate_ref, *refs):
    sources, (out_ref, held, sems) = refs[:-3], refs[-3:]
    count, subs = sources[-1].shape[:2]
    copies = []
    for k, src in enumerate(sources):
        src = src if src.shape[1] == subs else src.at[:, pl.ds(part * subs, subs), :]
        copies.append(pltpu.make_async_copy(src, held.at[pl.ds(k * count, count)], sems.at[k]))
    for copy in copies:
        copy.start()
    for copy in copies:
        copy.wait()

    def one_token(tok, carry):
        total = None
        for first in range(0, top_k, per_group):
            partial = None
            for j in range(first, first + per_group):
                scaled = held[pos_ref[tok * top_k + j]].astype(jnp.float32) * gate_ref[tok * top_k + j]
                partial = scaled if partial is None else partial + scaled
            partial = partial.astype(jnp.bfloat16).astype(jnp.float32)
            total = partial if total is None else total + partial
        out_ref[tok] = total.astype(jnp.bfloat16)
        return carry

    lax.fori_loop(0, out_ref.shape[0], one_token, 0, unroll=4)


def combine(pos, gates, sources, part, per_group):
    tokens_dev, top_k = pos.shape
    count, subs, _ = sources[-1].shape
    smem = pl.BlockSpec(memory_space=pltpu.SMEM)
    hbm = pl.BlockSpec(memory_space=pl.ANY)
    return pl.pallas_call(
        functools.partial(combine_kernel, per_group, top_k, part),
        in_specs=[smem, smem] + [hbm] * len(sources),
        out_specs=pl.BlockSpec(memory_space=pltpu.VMEM),
        out_shape=jax.ShapeDtypeStruct((tokens_dev, subs, LANES), jnp.bfloat16),
        scratch_shapes=[
            pltpu.VMEM((count * len(sources), subs, LANES), jnp.bfloat16),
            pltpu.SemaphoreType.DMA((len(sources),)),
        ],
        compiler_params=pltpu.CompilerParams(vmem_limit_bytes=60 * 2**20),
        cost_estimate=pl.CostEstimate(flops=0, bytes_accessed=2 * count * subs * LANES * len(sources), transcendentals=0),
    )(pos.reshape(-1), gates.reshape(-1), *sources)


def solution(mesh):
    groups = mesh.shape['grp']
    inner_size = mesh.shape['ing']
    row_spec = P(('dp', 'grp', 'ing'), None)
    weight_spec = P(('grp', 'ing'), None, None)
    ahead = [(i, (i + 1) % inner_size) for i in range(inner_size)]
    behind = [(i, (i - 1) % inner_size) for i in range(inner_size)]
    chip_ahead = [(g, (g + 2) % groups) for g in range(groups)]
    chip_behind = [(g, (g - 2) % groups) for g in range(groups)]
    partner = [(g, g ^ 1) for g in range(groups)]

    def device_step(tokens, expert_ids, gate_weights, w_gate, w_up, w_down):
        tokens_dev, dim = tokens.shape
        top_k = expert_ids.shape[1]
        local_exp = w_gate.shape[0]
        group_exp = local_exp * inner_size
        experts = group_exp * groups
        group_id = lax.axis_index('grp')
        per_group, expert_cap = cap_sizes(tokens_dev, top_k, groups, group_exp)
        inner = lax.axis_index('ing')

        first = w_gate[0]
        first, rest_gate, rest_up, rest_down = lax.optimization_barrier((first, w_gate, w_up, w_down))
        own = [(first if e == 0 else rest_gate[e], rest_up[e], rest_down[e]) for e in range(local_exp)]
        left = [tuple(lax.ppermute(w, 'ing', ahead) for w in own[e]) for e in range(local_exp)]
        right = [tuple(lax.ppermute(w, 'ing', behind) for w in own[e]) for e in range(local_exp)]
        far = []
        for e in range(local_exp):
            gate_w = lax.ppermute(left[e][0], 'ing', ahead)
            up_w = lax.ppermute(right[e][1], 'ing', behind)
            pieces = 2 if e < local_exp - 1 else 4
            width = dim // pieces
            downs = []
            for q in range(pieces):
                source, pairs = ((left, ahead), (right, behind))[q % 2]
                downs.append(lax.ppermute(source[e][2][:, q * width:(q + 1) * width], 'ing', pairs))
            far.append((gate_w, up_w, tuple(downs)))

        shifts = (0, -1, 1, 2)
        whole = lambda side: [(w[0], w[1], (w[2],)) for w in side]
        held = {0: whole(own), -1: whole(left), 1: whole(right), 2: far}
        phases = [(0, e) for e in range(local_exp)]
        phases += [(s, e) for e in range(local_exp) for s in (-1, 1)]
        phases += [(2, e) for e in range(local_exp)]
        assert inner_size == len(shifts)

        mid = tokens_dev // 2
        from_back = lax.ppermute(tokens, 'grp', chip_ahead)
        from_front = lax.ppermute(tokens, 'grp', chip_behind)
        across = [lax.ppermute(from_back[:mid], 'grp', chip_ahead), lax.ppermute(from_front[mid:], 'grp', chip_behind)]
        same_core = [tokens, from_back, from_front] + across
        rows_all = jnp.concatenate(same_core + [lax.ppermute(t, 'grp', partner) for t in same_core], axis=0)
        source_id = jnp.arange(groups, dtype=jnp.int32)
        chip_gap = (source_id // 2 - group_id // 2) % (groups // 2)
        block = jnp.where(chip_gap == 0, 0, jnp.where(chip_gap == groups // 2 - 1, 1, jnp.where(chip_gap == 1, 2, 3)))
        block = block + groups // 2 * (source_id % 2 != group_id % 2).astype(jnp.int32)
        assert groups // 2 == 4
        picked = jnp.any(expert_ids[:, :, None] == jnp.arange(experts), axis=1)
        before = jnp.tril(jnp.ones((tokens_dev, tokens_dev), jnp.bfloat16))
        upto = jnp.dot(before, picked.astype(jnp.bfloat16), preferred_element_type=jnp.float32).astype(jnp.int32)
        slot_tok = jnp.sum((upto.T[:, None, :] <= jnp.arange(expert_cap)[None, :, None]).astype(jnp.int32), axis=2)
        slot_tok = jnp.minimum(slot_tok, tokens_dev - 1).reshape(groups, group_exp * expert_cap)
        slot_in = lax.all_to_all(slot_tok, 'grp', 0, 0, tiled=True).reshape(groups, group_exp, expert_cap)
        slot_in = slot_in + (block * tokens_dev)[:, None, None]

        order = jnp.sum((expert_ids[:, None, :] < expert_ids[:, :, None]).astype(jnp.int32), axis=2)
        pick = order[:, :, None] == jnp.arange(top_k)
        ids = jnp.sum(jnp.where(pick, expert_ids[:, :, None], 0), axis=1)
        gates = jnp.sum(jnp.where(pick, gate_weights[:, :, None], 0.0), axis=1)
        rank = jnp.sum(jnp.where(ids[:, :, None] == jnp.arange(experts), upto[:, None, :], 0), axis=2) - 1
        member = ids % group_exp
        phase = jnp.zeros_like(ids)
        for p, (shift, e) in enumerate(phases):
            phase = jnp.where(member == (inner + shift) % inner_size * local_exp + e, p, phase)
        pos = (phase * groups + ids // group_exp) * expert_cap + rank

        returned = []
        for p, (shift, e) in enumerate(phases):
            which = (inner + shift) % inner_size * local_exp + e
            index = lax.dynamic_index_in_dim(slot_in, which, 1, keepdims=False).reshape(-1)
            rows = rows_all.at[index].get(mode='promise_in_bounds')
            gate_w, up_w, downs = held[shift][e]
            if p < len(phases) - 1:
                outs = [expert_ffn(rows, gate_w, up_w, downs, 256)]
            else:
                hidden = expert_hidden(rows, gate_w, up_w, 256)
                outs = []
                for part in range(2):
                    outs.append(expert_down(hidden, downs[2 * part:2 * part + 2], 256))
            backs = []
            for out in outs:
                subs = out.shape[1]
                back = lax.all_to_all(out.reshape(groups, expert_cap, subs, LANES), 'grp', 0, 0, tiled=True)
                backs.append(back.reshape(groups * expert_cap, subs, LANES))
            returned.append(backs)
        sources = [backs[0] for backs in returned[:-1]]
        sides = []
        for part, back in enumerate(returned[-1]):
            sides.append(combine(pos, gates, sources + [back], part, per_group))
        return jnp.concatenate([side.reshape(tokens_dev, dim // 2) for side in sides], axis=1)


    return jax.shard_map(device_step, mesh=mesh, in_specs=(row_spec, row_spec, row_spec, weight_spec, weight_spec, weight_spec), out_specs=row_spec, check_vma=False)
```

time: 1370 us -> 1270 us (0.927)
  waiting for transfers between devices: 783 us -> 612 us
  local copies, waits for them, and re-layouts: 208 us -> 255 us
  Pallas kernels: 252 us -> 273 us
    all_gather x1 -> x0, waiting for transfers between devices: 121 us -> none  [device_step(): rows_all = lax.all_gather(tokens, 'grp', tiled=True)]
    ppermute x24 -> x31, waiting for transfers between devices: 578 us -> 515 us  [the longest x6 260 us: device_step(): lax.ppermute(w, 'ing', ahead)]
    unnamed x25 -> x61, local copies, waits for them, and re-layouts: 6.37 us -> 48.5 us
    ppermute x24 -> x31, starting transfers between devices: 25.3 us -> 45.9 us  [the longest x6 11 us: device_step(): lax.ppermute(w, 'ing', behind)]
    pallas_call x9 -> x12, Pallas kernels: 252 us -> 273 us  [the longest x10 223 us: per_tile(): pl.pallas_call(kernel, grid=(count // tile,), in_specs=[pl.BlockSpec((til...]
    all_to_all x8 -> x9, waiting for transfers between devices: 83.1 us -> 97.9 us  [device_step(): lax.all_to_all(out.reshape(groups, expert_cap, subs, LANES), 'grp', 0, 0,...]
    all_to_all x8 -> x9, starting transfers between devices: 61.4 us -> 51 us  [device_step(): lax.all_to_all(out.reshape(groups, expert_cap, subs, LANES), 'grp', 0, 0,...]
  transfers between devices with their start and end apart: 34 -> 41, of which waited for: 15 -> 18; matrix products, arithmetic and copies ran while one was open for 14% -> 20% of each run, Pallas kernels for 14% -> 19%
where the time goes in v2:
time: 1270 us; the launch traced here: 1250 us
  waiting for transfers between devices  612 us (48%)
  Pallas kernels  273 us (21%)
  local copies, waits for them, and re-layouts  255 us (20%)
  starting transfers between devices  101 us (8%)
    ppermute x6, waiting for transfers between devices, device_step(): lax.ppermute(w, 'ing', ahead)  260 us
    pallas_call x10, Pallas kernels, per_tile(): pl.pallas_call(kernel, grid=(count // tile,), in_specs=[pl.BlockSpec((til...  223 us
    gather x8, local copies, waits for them, and re-layouts, device_step(): rows = rows_all.at[index].get(mode='promise_in_bounds')  168 us
    all_to_all x9, waiting for transfers between devices, device_step(): lax.all_to_all(out.reshape(groups, expert_cap, subs, LANES), 'grp', 0, 0,...  97.9 us
    ppermute x6, waiting for transfers between devices, device_step(): lax.ppermute(w, 'ing', behind)  89.7 us
    ppermute x1, waiting for transfers between devices, device_step(): from_back = lax.ppermute(tokens, 'grp', chip_ahead)  72.4 us
    ppermute x6, waiting for transfers between devices, device_step(): lax.ppermute(source[e][2][:, q * width:(q + 1) * width], 'ing', pairs)  71.2 us
    all_to_all x9, starting transfers between devices, device_step(): lax.all_to_all(out.reshape(groups, expert_cap, subs, LANES), 'grp', 0, 0,...  51 us
  transfers between devices with their start and end apart: 41, of which 18 were waited for; matrix products, arithmetic and copies ran while one was open for 20% of the time, Pallas kernels for 19%

profile of v2, /device:TPU:97, one launch (start us, length us, event | category | flops | bytes accessed | tf_op | source)
XLA Modules:
  0.0 1253.8 jit_solution(4775219931541491398)
XLA Ops:
  21.3 72.4 %collective-permute-done = bf16[1024,2048]{1,0:T(8,128)(2,1)} collective-permute-done((bf16[1024,2048]{1,0:T(8,128)(2,1)}, bf16[1024,2048]{1,0:T(8,128)(2,1)}, u32[]{:S(2)}, u32[]{:S(2)}) %collective-permute-start) | collective-permute-done | bytes 4194336 | tf_op jit(solution)/shard_map/ppermute | solution.py:172
  110.3 85.5 %collective-permute-done.17.refs_0_ = bf16[1024,2048]{1,0:T(8,128)(2,1)S(1)} collective-permute-done((bf16[1024,2048]{1,0:T(8,128)(2,1)}, bf16[1024,2048]{1,0:T(8,128)(2,1)S(1)}, u32[]{:S(2)}, u32[]{:S(2)}) %collective-permute-start.17) | collective-permute-done | bytes 4194336 | tf_op jit(solution)/shard_map/ppermute | solution.py:149
  210.1 67.3 %collective-permute-done.20.refs_0_ = bf16[1024,2048]{1,0:T(8,128)(2,1)} collective-permute-done((bf16[1024,2048]{1,0:T(8,128)(2,1)}, bf16[1024,2048]{1,0:T(8,128)(2,1)}, u32[]{:S(2)}, u32[]{:S(2)}) %collective-permute-start.20) | collective-permute-done | bytes 4194336 | tf_op jit(solution)/shard_map/ppermute | solution.py:150
  327.8 21.0 %gather_fusion.7 = bf16[1536,2048]{1,0:T(8,128)(2,1)} fusion(bf16[8192,2048]{1,0:T(8,128)(2,1)} %constant_dynamic-update-slice_fusion, s32[2048]{0:T(1024)S(1)} %pad_clamp_fusion), kind=kCustom, calls=%fused_computation.7 | custom fusion | bytes 12589056 | tf_op jit(solution)/shard_map/gather | solution.py:205
  348.7 21.2 %collective-permute-done.25.gate_ref = bf16[2048,1024]{1,0:T(8,128)(2,1)} collective-permute-done((bf16[2048,1024]{1,0:T(8,128)(2,1)}, bf16[2048,1024]{1,0:T(8,128)(2,1)}, u32[]{:S(2)}, u32[]{:S(2)}) %collective-permute-start.25) | collective-permute-done | bytes 4194336 | tf_op jit(solution)/shard_map/ppermute | solution.py:153
  369.9 18.7 %shard_map.71.x_ref = bf16[1536,1024]{1,0:T(8,128)(2,1)} custom-call(bf16[1536,2048]{1,0:T(8,128)(2,1)} %gather_fusion.7, bf16[2048,1024]{1,0:T(8,128)(2,1)} %collective-permute-done.25.gate_ref, bf16[2048,1024]{1,0:T(8,128)(2,1)} %collective-permute-done.26.up_ref), custom_call_target="tpu_custom_call" | custom-call | flops 12884901888 | bytes 17825792 | tf_op jit(solution)/shard_map/pallas_call | solution.py:56
  408.9 20.9 %gather_fusion = bf16[1536,2048]{1,0:T(8,128)(2,1)} fusion(bf16[8192,2048]{1,0:T(8,128)(2,1)} %constant_dynamic-update-slice_fusion, s32[2048]{0:T(1024)S(1)} %get-tuple-element.30), kind=kCustom, calls=%fused_computation | custom fusion | bytes 12589056 | tf_op jit(solution)/shard_map/gather | solution.py:205
  429.8 26.6 %shard_map.64 = bf16[1536,16,128]{2,1,0:T(8,128)(2,1)} custom-call(bf16[1536,2048]{1,0:T(8,128)(2,1)} %gather_fusion, bf16[2048,1024]{1,0:T(8,128)(2,1)} %slice_bitcast_fusion.5.gate_ref, bf16[2048,1024]{1,0:T(8,128)(2,1)} %get-tuple-element.24.up_ref, bf16[1024,2048]{1,0:T(8,128)(2,1)} %get-tuple-element.22.refs_0_), custom_call_target="tpu_custom_call" | custom-call | flops 19327352832 | bytes 25165824 | tf_op jit(solution)/shard_map/pallas_call | solution.py:56
  466.7 21.0 %gather_fusion.1 = bf16[1536,2048]{1,0:T(8,128)(2,1)} fusion(bf16[8192,2048]{1,0:T(8,128)(2,1)} %constant_dynamic-update-slice_fusion, s32[2048]{0:T(1024)S(1)} %get-tuple-element.29), kind=kCustom, calls=%fused_computation.1 | custom fusion | bytes 12589056 | tf_op jit(solution)/shard_map/gather | solution.py:205
  487.7 26.6 %shard_map.65 = bf16[1536,16,128]{2,1,0:T(8,128)(2,1)} custom-call(bf16[1536,2048]{1,0:T(8,128)(2,1)} %gather_fusion.1, bf16[2048,1024]{1,0:T(8,128)(2,1)} %copy-done.4, bf16[2048,1024]{1,0:T(8,128)(2,1)} %copy-done.5, bf16[1024,2048]{1,0:T(8,128)(2,1)} %get-tuple-element.21.refs_0_), custom_call_target="tpu_custom_call" | custom-call | flops 19327352832 | bytes 25165824 | tf_op jit(solution)/shard_map/pallas_call | solution.py:56
  514.3 20.2 %all-to-all-done.1 = bf16[8,192,16,128]{3,2,1,0:T(8,128)(2,1)} async-done(((bf16[8,192,16,128]{3,2,1,0:T(8,128)(2,1)}), bf16[8,192,16,128]{3,2,1,0:T(8,128)(2,1)}, u32[]{:S(2)}, u32[]{:S(2)}) %all-to-all-start.1) | async-done | bytes 6291488 | tf_op jit(solution)/shard_map/all_to_all | solution.py:217
  543.4 21.0 %gather_fusion.2 = bf16[1536,2048]{1,0:T(8,128)(2,1)} fusion(bf16[8192,2048]{1,0:T(8,128)(2,1)} %constant_dynamic-update-slice_fusion, s32[2048]{0:T(1024)S(1)} %pad_clamp_fusion.5), kind=kCustom, calls=%fused_computation.2 | custom fusion | bytes 12589056 | tf_op jit(solution)/shard_map/gather | solution.py:205
  564.5 82.0 %collective-permute-done.10.up_ref = bf16[2048,1024]{1,0:T(8,128)(2,1)} collective-permute-done((bf16[2048,1024]{1,0:T(8,128)(2,1)}, bf16[2048,1024]{1,0:T(8,128)(2,1)}, u32[]{:S(2)}, u32[]{:S(2)}) %collective-permute-start.10) | collective-permute-done | bytes 4194336 | tf_op jit(solution)/shard_map/ppermute | solution.py:149
  646.5 89.9 %collective-permute-done.11.refs_0_ = bf16[1024,2048]{1,0:T(8,128)(2,1)} collective-permute-done((bf16[1024,2048]{1,0:T(8,128)(2,1)}, bf16[1024,2048]{1,0:T(8,128)(2,1)}, u32[]{:S(2)}, u32[]{:S(2)}) %collective-permute-start.11) | collective-permute-done | bytes 4194336 | tf_op jit(solution)/shard_map/ppermute | solution.py:149
  736.4 26.7 %shard_map.66 = bf16[1536,16,128]{2,1,0:T(8,128)(2,1)} custom-call(bf16[1536,2048]{1,0:T(8,128)(2,1)} %gather_fusion.2, bf16[2048,1024]{1,0:T(8,128)(2,1)} %collective-permute-done.9.gate_ref, bf16[2048,1024]{1,0:T(8,128)(2,1)} %collective-permute-done.10.up_ref, bf16[1024,2048]{1,0:T(8,128)(2,1)} %collective-permute-done.11.refs_0_), custom_call_target="tpu_custom_call" | custom-call | flops 19327352832 | bytes 25165824 | tf_op jit(solution)/shard_map/pallas_call | solution.py:56
  769.1 20.8 %gather_fusion.3 = bf16[1536,2048]{1,0:T(8,128)(2,1)} fusion(bf16[8192,2048]{1,0:T(8,128)(2,1)} %constant_dynamic-update-slice_fusion, s32[2048]{0:T(1024)S(1)} %pad_clamp_fusion.4), kind=kCustom, calls=%fused_computation.3 | custom fusion | bytes 12589056 | tf_op jit(solution)/shard_map/gather | solution.py:205
  789.9 22.5 %collective-permute-done.14.refs_0_ = bf16[1024,2048]{1,0:T(8,128)(2,1)} collective-permute-done((bf16[1024,2048]{1,0:T(8,128)(2,1)}, bf16[1024,2048]{1,0:T(8,128)(2,1)}, u32[]{:S(2)}, u32[]{:S(2)}) %collective-permute-start.14) | collective-permute-done | bytes 4194336 | tf_op jit(solution)/shard_map/ppermute | solution.py:150
  812.4 26.6 %shard_map.67 = bf16[1536,16,128]{2,1,0:T(8,128)(2,1)} custom-call(bf16[1536,2048]{1,0:T(8,128)(2,1)} %gather_fusion.3, bf16[2048,1024]{1,0:T(8,128)(2,1)} %collective-permute-done.12.gate_ref, bf16[2048,1024]{1,0:T(8,128)(2,1)} %collective-permute-done.13.up_ref, bf16[1024,2048]{1,0:T(8,128)(2,1)} %collective-permute-done.14.refs_0_), custom_call_target="tpu_custom_call" | custom-call | flops 19327352832 | bytes 25165824 | tf_op jit(solution)/shard_map/pallas_call | solution.py:56
  848.8 21.0 %gather_fusion.4 = bf16[1536,2048]{1,0:T(8,128)(2,1)} fusion(bf16[8192,2048]{1,0:T(8,128)(2,1)} %constant_dynamic-update-slice_fusion, s32[2048]{0:T(1024)S(1)} %pad_clamp_fusion.3), kind=kCustom, calls=%fused_computation.4 | custom fusion | bytes 12589056 | tf_op jit(solution)/shard_map/gather | solution.py:205
  869.8 26.6 %shard_map.68 = bf16[1536,16,128]{2,1,0:T(8,128)(2,1)} custom-call(bf16[1536,2048]{1,0:T(8,128)(2,1)} %gather_fusion.4, bf16[2048,1024]{1,0:T(8,128)(2,1)} %collective-permute-done.15.gate_ref, bf16[2048,1024]{1,0:T(8,128)(2,1)} %collective-permute-done.16.up_ref, bf16[1024,2048]{1,0:T(8,128)(2,1)} %copy-done.8), custom_call_target="tpu_custom_call" | custom-call | flops 19327352832 | bytes 25165824 | tf_op jit(solution)/shard_map/pallas_call | solution.py:56
  896.5 20.8 %all-to-all-done.4 = bf16[8,192,16,128]{3,2,1,0:T(8,128)(2,1)} async-done(((bf16[8,192,16,128]{3,2,1,0:T(8,128)(2,1)}), bf16[8,192,16,128]{3,2,1,0:T(8,128)(2,1)}, u32[]{:S(2)}, u32[]{:S(2)}) %all-to-all-start.4) | async-done | bytes 6291488 | tf_op jit(solution)/shard_map/all_to_all | solution.py:217
  925.9 20.9 %gather_fusion.5 = bf16[1536,2048]{1,0:T(8,128)(2,1)} fusion(bf16[8192,2048]{1,0:T(8,128)(2,1)} %constant_dynamic-update-slice_fusion, s32[2048]{0:T(1024)S(1)} %pad_clamp_fusion.2), kind=kCustom, calls=%fused_computation.5 | custom fusion | bytes 12589056 | tf_op jit(solution)/shard_map/gather | solution.py:205
  946.8 26.6 %shard_map.69 = bf16[1536,16,128]{2,1,0:T(8,128)(2,1)} custom-call(bf16[1536,2048]{1,0:T(8,128)(2,1)} %gather_fusion.5, bf16[2048,1024]{1,0:T(8,128)(2,1)} %collective-permute-done.18.gate_ref, bf16[2048,1024]{1,0:T(8,128)(2,1)} %copy-done.19, bf16[1024,2048]{1,0:T(8,128)(2,1)} %collective-permute-done.20.refs_0_), custom_call_target="tpu_custom_call" | custom-call | flops 19327352832 | bytes 25165824 | tf_op jit(solution)/shard_map/pallas_call | solution.py:56
  973.4 20.9 %all-to-all-done.5 = bf16[8,192,16,128]{3,2,1,0:T(8,128)(2,1)} async-done(((bf16[8,192,16,128]{3,2,1,0:T(8,128)(2,1)}), bf16[8,192,16,128]{3,2,1,0:T(8,128)(2,1)}, u32[]{:S(2)}, u32[]{:S(2)}) %all-to-all-start.5) | async-done | bytes 6291488 | tf_op jit(solution)/shard_map/all_to_all | solution.py:217
  1007.9 20.9 %gather_fusion.6 = bf16[1536,2048]{1,0:T(8,128)(2,1)} fusion(bf16[8192,2048]{1,0:T(8,128)(2,1)} %constant_dynamic-update-slice_fusion, s32[2048]{0:T(1024)S(1)} %pad_clamp_fusion.1), kind=kCustom, calls=%fused_computation.6 | custom fusion | bytes 12589056 | tf_op jit(solution)/shard_map/gather | solution.py:205
  1028.9 32.6 %collective-permute-done.23.refs_0_ = bf16[1024,1024]{1,0:T(8,128)(2,1)} collective-permute-done((bf16[1024,1024]{1,0:T(8,128)(2,1)S(1)}, bf16[1024,1024]{1,0:T(8,128)(2,1)}, u32[]{:S(2)}, u32[]{:S(2)}) %collective-permute-start.23) | collective-permute-done | bytes 2097184 | tf_op jit(solution)/shard_map/ppermute | solution.py:160
  1061.5 11.9 collective-permute-done.24.refs_1_
  1073.3 27.5 %shard_map.70 = bf16[1536,16,128]{2,1,0:T(8,128)(2,1)} custom-call(bf16[1536,2048]{1,0:T(8,128)(2,1)} %gather_fusion.6, bf16[2048,1024]{1,0:T(8,128)(2,1)} %collective-permute-done.21.gate_ref, bf16[2048,1024]{1,0:T(8,128)(2,1)} %collective-permute-done.22.up_ref, bf16[1024,1024]{1,0:T(8,128)(2,1)} %collective-permute-done.23.refs_0_, ...), custom_call_target="tpu_custom_call" | custom-call | flops 19327352832 | bytes 25165824 | tf_op jit(solution)/shard_map/pallas_call | solution.py:56
  1110.4 23.0 %collective-permute-done.27.refs_0_ = bf16[1024,512]{1,0:T(8,128)(2,1)S(1)} collective-permute-done((bf16[1024,512]{1,0:T(8,128)(2,1)S(1)}, bf16[1024,512]{1,0:T(8,128)(2,1)S(1)}, u32[]{:S(2)}, u32[]{:S(2)}) %collective-permute-start.27) | collective-permute-done | bytes 1048608 | tf_op jit(solution)/shard_map/ppermute | solution.py:160
  1143.8 34.4 %all-to-all-done.7 = bf16[8,192,16,128]{3,2,1,0:T(8,128)(2,1)} async-done(((bf16[8,192,16,128]{3,2,1,0:T(8,128)(2,1)}), bf16[8,192,16,128]{3,2,1,0:T(8,128)(2,1)}, u32[]{:S(2)}, u32[]{:S(2)}) %all-to-all-start.7) | async-done | bytes 6291488 | tf_op jit(solution)/shard_map/all_to_all | solution.py:217
  1191.4 25.0 %shard_map.75 = bf16[1024,8,128]{2,1,0:T(8,128)(2,1)} custom-call(s32[8192]{0:T(1024)} %fusion.11.pos_ref, f32[8192]{0:T(1024)} %reshape.395.gate_ref, bf16[1536,16,128]{2,1,0:T(8,128)(2,1)} %bitcast.5.refs_0_, bf16[1536,16,128]{2,1,0:T(8,128)(2,1)} %bitcast.10.refs_1_, bf16[1536,16,128]{2,1,0:T(8,128)(2,1)} %bitcast.12.refs_2_, ...), custom_call_target="tpu_custom_call" | custom-call | bytes 25165824 | tf_op jit(solution)/shard_map/pallas_call | solution.py:111
  1222.0 25.0 %shard_map.73 = bf16[1024,8,128]{2,1,0:T(8,128)(2,1)} custom-call(s32[8192]{0:T(1024)} %fusion.11.pos_ref, f32[8192]{0:T(1024)} %reshape.395.gate_ref, bf16[1536,16,128]{2,1,0:T(8,128)(2,1)} %bitcast.5.refs_0_, bf16[1536,16,128]{2,1,0:T(8,128)(2,1)} %bitcast.10.refs_1_, bf16[1536,16,128]{2,1,0:T(8,128)(2,1)} %bitcast.12.refs_2_, ...), custom_call_target="tpu_custom_call" | custom-call | bytes 25165824 | tf_op jit(solution)/shard_map/pallas_call | solution.py:111
  (189 shorter events, 224.7 us)
Async XLA Ops:
  0.0 93.7 %collective-permute-start = (bf16[1024,2048]{1,0:T(8,128)(2,1)}, bf16[1024,2048]{1,0:T(8,128)(2,1)}, u32[]{:S(2)}, u32[]{:S(2)}) collective-permute-start(bf16[1024,2048]{1,0:T(8,128)(2,1)} %param.6), channel_id=1, source_target_pairs={{0,2},{1,3},{2,4},{3,5},{4,6},{5,7},{6,0},{7,1},{8,10},{9,11},{10,... | collective-permute-start | bytes 12582920 | tf_op jit(solution)/shard_map/ppermute | solution.py:172
  2.2 96.5 %collective-permute-start.1 = (bf16[1024,2048]{1,0:T(8,128)(2,1)}, bf16[1024,2048]{1,0:T(8,128)(2,1)}, u32[]{:S(2)}, u32[]{:S(2)}) collective-permute-start(bf16[1024,2048]{1,0:T(8,128)(2,1)} %param.6), channel_id=1, source_target_pairs={{0,6},{1,7},{2,0},{3,1},{4,2},{5,3},{6,4},{7,5},{8,14},{9,15},{10,... | collective-permute-start | bytes 12582920 | tf_op jit(solution)/shard_map/ppermute | solution.py:173
  3.8 94.9 %collective-permute-start.4 = (bf16[1024,2048]{1,0:T(8,128)(2,1)}, bf16[1024,2048]{1,0:T(8,128)(2,1)}, u32[]{:S(2)}, u32[]{:S(2)}) collective-permute-start(bf16[1024,2048]{1,0:T(8,128)(2,1)} %param.6), channel_id=1, source_target_pairs={{0,1},{1,0},{2,3},{3,2},{4,5},{5,4},{6,7},{7,6},{8,9},{9,8},{10,11... | collective-permute-start | bytes 12582920 | tf_op jit(solution)/shard_map/ppermute | solution.py:176
  10.4 95.7 %collective-permute-start.15 = (bf16[2048,1024]{1,0:T(8,128)(2,1)S(1)}, bf16[2048,1024]{1,0:T(8,128)(2,1)}, u32[]{:S(2)}, u32[]{:S(2)}) collective-permute-start(bf16[2048,1024]{1,0:T(8,128)(2,1)S(1)} %slice_bitcast_fusion.2.gate_ref), channel_id=1, source_target_pairs={{0,8},{8,16},{16,24},{24,0},{1,9},{9,17},{17,25},{25,1},{2,10},{10... | collective-permute-start | bytes 12582920 | tf_op jit(solution)/shard_map/ppermute | solution.py:149
  16.8 179.1 %collective-permute-start.17 = (bf16[1024,2048]{1,0:T(8,128)(2,1)}, bf16[1024,2048]{1,0:T(8,128)(2,1)S(1)}, u32[]{:S(2)}, u32[]{:S(2)}) collective-permute-start(bf16[1024,2048]{1,0:T(8,128)(2,1)} %get-tuple-element.21.refs_0_), channel_id=1, source_target_pairs={{0,8},{8,16},{16,24},{24,0},{1,9},{9,17},{17,25},{25,1},{2,10},{10... | collective-permute-start | bytes 12582920 | tf_op jit(solution)/shard_map/ppermute | solution.py:149
  93.7 103.7 %collective-permute-start.19 = (bf16[2048,1024]{1,0:T(8,128)(2,1)S(1)}, bf16[2048,1024]{1,0:T(8,128)(2,1)S(1)}, u32[]{:S(2)}, u32[]{:S(2)}) collective-permute-start(bf16[2048,1024]{1,0:T(8,128)(2,1)S(1)} %get-tuple-element.23.up_ref), channel_id=1, source_target_pairs={{0,24},{8,0},{16,8},{24,16},{1,25},{9,1},{17,9},{25,17},{2,26},{10... | collective-permute-start | bytes 12582920 | tf_op jit(solution)/shard_map/ppermute | solution.py:150
  98.7 178.7 %collective-permute-start.20 = (bf16[1024,2048]{1,0:T(8,128)(2,1)}, bf16[1024,2048]{1,0:T(8,128)(2,1)}, u32[]{:S(2)}, u32[]{:S(2)}) collective-permute-start(bf16[1024,2048]{1,0:T(8,128)(2,1)} %get-tuple-element.21.refs_0_), channel_id=1, source_target_pairs={{0,24},{8,0},{16,8},{24,16},{1,25},{9,1},{17,9},{25,17},{2,26},{10... | collective-permute-start | bytes 12582920 | tf_op jit(solution)/shard_map/ppermute | solution.py:150
  98.7 201.5 %collective-permute-start.5 = (bf16[1024,2048]{1,0:T(8,128)(2,1)}, bf16[1024,2048]{1,0:T(8,128)(2,1)}, u32[]{:S(2)}, u32[]{:S(2)}) collective-permute-start(bf16[1024,2048]{1,0:T(8,128)(2,1)} %collective-permute-done), channel_id=1, source_target_pairs={{0,1},{1,0},{2,3},{3,2},{4,5},{5,4},{6,7},{7,6},{8,9},{9,8},{10,11... | collective-permute-start | bytes 12582920 | tf_op jit(solution)/shard_map/ppermute | solution.py:176
  106.1 171.6 %collective-permute-start.2 = (bf16[512,2048]{1,0:T(8,128)(2,1)}, bf16[512,2048]{1,0:T(8,128)(2,1)S(1)}, u32[]{:S(2)}, u32[]{:S(2)}) collective-permute-start(bf16[512,2048]{1,0:T(8,128)(2,1)} %slice.72), channel_id=1, source_target_pairs={{0,2},{1,3},{2,4},{3,5},{4,6},{5,7},{6,0},{7,1},{8,10},{9,11},{10,... | collective-permute-start | bytes 6291464 | tf_op jit(solution)/shard_map/ppermute | solution.py:174
  195.9 100.8 %collective-permute-start.3 = (bf16[512,2048]{1,0:T(8,128)(2,1)}, bf16[512,2048]{1,0:T(8,128)(2,1)}, u32[]{:S(2)}, u32[]{:S(2)}) collective-permute-start(bf16[512,2048]{1,0:T(8,128)(2,1)} %slice.73), channel_id=1, source_target_pairs={{0,6},{1,7},{2,0},{3,1},{4,2},{5,3},{6,4},{7,5},{8,14},{9,15},{10,... | collective-permute-start | bytes 6291464 | tf_op jit(solution)/shard_map/ppermute | solution.py:174
  197.8 119.6 %collective-permute-start.6 = (bf16[1024,2048]{1,0:T(8,128)(2,1)}, bf16[1024,2048]{1,0:T(8,128)(2,1)}, u32[]{:S(2)}, u32[]{:S(2)}) collective-permute-start(bf16[1024,2048]{1,0:T(8,128)(2,1)} %collective-permute-done.1), channel_id=1, source_target_pairs={{0,1},{1,0},{2,3},{3,2},{4,5},{5,4},{6,7},{7,6},{8,9},{9,8},{10,11... | collective-permute-start | bytes 12582920 | tf_op jit(solution)/shard_map/ppermute | solution.py:176
  206.2 79.7 %all-to-all-start = ((s32[8,1,1536]{2,1,0:T(1,128)}), s32[8,1,1536]{2,1,0:T(1,128)S(1)}, u32[]{:S(2)}, u32[]{:S(2)}) async-start(s32[8,1,1536]{2,1,0:T(1,128)} %min.20), calls=%async_computation | async-start | bytes 98304 | tf_op jit(solution)/shard_map/all_to_all | solution.py:187
  277.4 92.6 %collective-permute-start.25 = (bf16[2048,1024]{1,0:T(8,128)(2,1)}, bf16[2048,1024]{1,0:T(8,128)(2,1)}, u32[]{:S(2)}, u32[]{:S(2)}) collective-permute-start(bf16[2048,1024]{1,0:T(8,128)(2,1)} %collective-permute-done.15.gate_ref), channel_id=1, source_target_pairs={{0,8},{8,16},{16,24},{24,0},{1,9},{9,17},{17,25},{25,1},{2,10},{10... | collective-permute-start | bytes 12582920 | tf_op jit(solution)/shard_map/ppermute | solution.py:153
  277.7 92.2 %collective-permute-start.26 = (bf16[2048,1024]{1,0:T(8,128)(2,1)}, bf16[2048,1024]{1,0:T(8,128)(2,1)}, u32[]{:S(2)}, u32[]{:S(2)}) collective-permute-start(bf16[2048,1024]{1,0:T(8,128)(2,1)} %copy-done.19), channel_id=1, source_target_pairs={{0,24},{8,0},{16,8},{24,16},{1,25},{9,1},{17,9},{25,17},{2,26},{10... | collective-permute-start | bytes 12582920 | tf_op jit(solution)/shard_map/ppermute | solution.py:154
  317.4 75.0 %collective-permute-start.29 = (bf16[1024,512]{1,0:T(8,128)(2,1)S(1)}, bf16[1024,512]{1,0:T(8,128)(2,1)}, u32[]{:S(2)}, u32[]{:S(2)}) collective-permute-start(bf16[1024,512]{1,0:T(8,128)(2,1)S(1)} %get-tuple-element.28), channel_id=1, source_target_pairs={{0,8},{8,16},{16,24},{24,0},{1,9},{9,17},{17,25},{25,1},{2,10},{10... | collective-permute-start | bytes 3145736 | tf_op jit(solution)/shard_map/ppermute | solution.py:160
  458.0 76.5 %all-to-all-start.1 = ((bf16[8,192,16,128]{3,2,1,0:T(8,128)(2,1)}), bf16[8,192,16,128]{3,2,1,0:T(8,128)(2,1)}, u32[]{:S(2)}, u32[]{:S(2)}) async-start(bf16[8,192,16,128]{3,2,1,0:T(8,128)(2,1)} %bitcast.54), calls=%async_computation.1 | async-start | bytes 12582912 | tf_op jit(solution)/shard_map/all_to_all | solution.py:217
  463.1 101.3 %collective-permute-start.9 = (bf16[2048,1024]{1,0:T(8,128)(2,1)}, bf16[2048,1024]{1,0:T(8,128)(2,1)}, u32[]{:S(2)}, u32[]{:S(2)}) collective-permute-start(bf16[2048,1024]{1,0:T(8,128)(2,1)} %slice_bitcast_fusion.5.gate_ref), channel_id=1, source_target_pairs={{0,8},{8,16},{16,24},{24,0},{1,9},{9,17},{17,25},{25,1},{2,10},{10... | collective-permute-start | bytes 12582920 | tf_op jit(solution)/shard_map/ppermute | solution.py:149
  464.0 182.5 %collective-permute-start.10 = (bf16[2048,1024]{1,0:T(8,128)(2,1)}, bf16[2048,1024]{1,0:T(8,128)(2,1)}, u32[]{:S(2)}, u32[]{:S(2)}) collective-permute-start(bf16[2048,1024]{1,0:T(8,128)(2,1)} %get-tuple-element.24.up_ref), channel_id=1, source_target_pairs={{0,8},{8,16},{16,24},{24,0},{1,9},{9,17},{17,25},{25,1},{2,10},{10... | collective-permute-start | bytes 12582920 | tf_op jit(solution)/shard_map/ppermute | solution.py:149
  465.5 270.9 %collective-permute-start.11 = (bf16[1024,2048]{1,0:T(8,128)(2,1)}, bf16[1024,2048]{1,0:T(8,128)(2,1)}, u32[]{:S(2)}, u32[]{:S(2)}) collective-permute-start(bf16[1024,2048]{1,0:T(8,128)(2,1)} %get-tuple-element.22.refs_0_), channel_id=1, source_target_pairs={{0,8},{8,16},{16,24},{24,0},{1,9},{9,17},{17,25},{25,1},{2,10},{10... | collective-permute-start | bytes 12582920 | tf_op jit(solution)/shard_map/ppermute | solution.py:149
  534.5 228.5 %all-to-all-start.2 = ((bf16[8,192,16,128]{3,2,1,0:T(8,128)(2,1)}), bf16[8,192,16,128]{3,2,1,0:T(8,128)(2,1)}, u32[]{:S(2)}, u32[]{:S(2)}) async-start(bf16[8,192,16,128]{3,2,1,0:T(8,128)(2,1)} %bitcast.49), calls=%async_computation.2 | async-start | bytes 12582912 | tf_op jit(solution)/shard_map/all_to_all | solution.py:217
  540.1 249.8 %collective-permute-start.12 = (bf16[2048,1024]{1,0:T(8,128)(2,1)}, bf16[2048,1024]{1,0:T(8,128)(2,1)}, u32[]{:S(2)}, u32[]{:S(2)}) collective-permute-start(bf16[2048,1024]{1,0:T(8,128)(2,1)} %slice_bitcast_fusion.5.gate_ref), channel_id=1, source_target_pairs={{0,24},{8,0},{16,8},{24,16},{1,25},{9,1},{17,9},{25,17},{2,26},{10... | collective-permute-start | bytes 12582920 | tf_op jit(solution)/shard_map/ppermute | solution.py:150
  542.7 247.2 %collective-permute-start.13 = (bf16[2048,1024]{1,0:T(8,128)(2,1)}, bf16[2048,1024]{1,0:T(8,128)(2,1)}, u32[]{:S(2)}, u32[]{:S(2)}) collective-permute-start(bf16[2048,1024]{1,0:T(8,128)(2,1)} %get-tuple-element.24.up_ref), channel_id=1, source_target_pairs={{0,24},{8,0},{16,8},{24,16},{1,25},{9,1},{17,9},{25,17},{2,26},{10... | collective-permute-start | bytes 12582920 | tf_op jit(solution)/shard_map/ppermute | solution.py:150
  564.5 247.9 %collective-permute-start.14 = (bf16[1024,2048]{1,0:T(8,128)(2,1)}, bf16[1024,2048]{1,0:T(8,128)(2,1)}, u32[]{:S(2)}, u32[]{:S(2)}) collective-permute-start(bf16[1024,2048]{1,0:T(8,128)(2,1)} %get-tuple-element.22.refs_0_), channel_id=1, source_target_pairs={{0,24},{8,0},{16,8},{24,16},{1,25},{9,1},{17,9},{25,17},{2,26},{10... | collective-permute-start | bytes 12582920 | tf_op jit(solution)/shard_map/ppermute | solution.py:150
  763.1 77.1 %all-to-all-start.3 = ((bf16[8,192,16,128]{3,2,1,0:T(8,128)(2,1)}), bf16[8,192,16,128]{3,2,1,0:T(8,128)(2,1)}, u32[]{:S(2)}, u32[]{:S(2)}) async-start(bf16[8,192,16,128]{3,2,1,0:T(8,128)(2,1)} %bitcast.50), calls=%async_computation.3 | async-start | bytes 12582912 | tf_op jit(solution)/shard_map/all_to_all | solution.py:217
  768.9 100.9 %collective-permute-start.16 = (bf16[2048,1024]{1,0:T(8,128)(2,1)}, bf16[2048,1024]{1,0:T(8,128)(2,1)}, u32[]{:S(2)}, u32[]{:S(2)}) collective-permute-start(bf16[2048,1024]{1,0:T(8,128)(2,1)} %copy-done.5), channel_id=1, source_target_pairs={{0,8},{8,16},{16,24},{24,0},{1,9},{9,17},{17,25},{25,1},{2,10},{10... | collective-permute-start | bytes 12582920 | tf_op jit(solution)/shard_map/ppermute | solution.py:149
  840.2 77.1 %all-to-all-start.4 = ((bf16[8,192,16,128]{3,2,1,0:T(8,128)(2,1)}), bf16[8,192,16,128]{3,2,1,0:T(8,128)(2,1)}, u32[]{:S(2)}, u32[]{:S(2)}) async-start(bf16[8,192,16,128]{3,2,1,0:T(8,128)(2,1)} %bitcast.53), calls=%async_computation.4 | async-start | bytes 12582912 | tf_op jit(solution)/shard_map/all_to_all | solution.py:217
  845.9 100.9 %collective-permute-start.18 = (bf16[2048,1024]{1,0:T(8,128)(2,1)}, bf16[2048,1024]{1,0:T(8,128)(2,1)}, u32[]{:S(2)}, u32[]{:S(2)}) collective-permute-start(bf16[2048,1024]{1,0:T(8,128)(2,1)} %copy-done.4), channel_id=1, source_target_pairs={{0,24},{8,0},{16,8},{24,16},{1,25},{9,1},{17,9},{25,17},{2,26},{10... | collective-permute-start | bytes 12582920 | tf_op jit(solution)/shard_map/ppermute | solution.py:150
  917.3 77.1 %all-to-all-start.5 = ((bf16[8,192,16,128]{3,2,1,0:T(8,128)(2,1)}), bf16[8,192,16,128]{3,2,1,0:T(8,128)(2,1)}, u32[]{:S(2)}, u32[]{:S(2)}) async-start(bf16[8,192,16,128]{3,2,1,0:T(8,128)(2,1)} %bitcast.51), calls=%async_computation.5 | async-start | bytes 12582912 | tf_op jit(solution)/shard_map/all_to_all | solution.py:217
  923.1 150.2 %collective-permute-start.21 = (bf16[2048,1024]{1,0:T(8,128)(2,1)}, bf16[2048,1024]{1,0:T(8,128)(2,1)}, u32[]{:S(2)}, u32[]{:S(2)}) collective-permute-start(bf16[2048,1024]{1,0:T(8,128)(2,1)} %collective-permute-done.9.gate_ref), channel_id=1, source_target_pairs={{0,8},{8,16},{16,24},{24,0},{1,9},{9,17},{17,25},{25,1},{2,10},{10... | collective-permute-start | bytes 12582920 | tf_op jit(solution)/shard_map/ppermute | solution.py:153
  923.2 150.1 %collective-permute-start.22 = (bf16[2048,1024]{1,0:T(8,128)(2,1)}, bf16[2048,1024]{1,0:T(8,128)(2,1)}, u32[]{:S(2)}, u32[]{:S(2)}) collective-permute-start(bf16[2048,1024]{1,0:T(8,128)(2,1)} %collective-permute-done.13.up_ref), channel_id=1, source_target_pairs={{0,24},{8,0},{16,8},{24,16},{1,25},{9,1},{17,9},{25,17},{2,26},{10... | collective-permute-start | bytes 12582920 | tf_op jit(solution)/shard_map/ppermute | solution.py:154
  994.3 106.5 %all-to-all-start.6 = ((bf16[8,192,16,128]{3,2,1,0:T(8,128)(2,1)}), bf16[8,192,16,128]{3,2,1,0:T(8,128)(2,1)}, u32[]{:S(2)}, u32[]{:S(2)}) async-start(bf16[8,192,16,128]{3,2,1,0:T(8,128)(2,1)} %bitcast.48), calls=%async_computation.6 | async-start | bytes 12582912 | tf_op jit(solution)/shard_map/all_to_all | solution.py:217
  1100.8 77.4 %all-to-all-start.7 = ((bf16[8,192,16,128]{3,2,1,0:T(8,128)(2,1)}), bf16[8,192,16,128]{3,2,1,0:T(8,128)(2,1)}, u32[]{:S(2)}, u32[]{:S(2)}) async-start(bf16[8,192,16,128]{3,2,1,0:T(8,128)(2,1)} %bitcast.52), calls=%async_computation.7 | async-start | bytes 12582912 | tf_op jit(solution)/shard_map/all_to_all | solution.py:217
  (34 other events, 1016.1 us)

commit v3 on v2

--- a/solution.py
+++ b/solution.py
@@ -48,15 +48,22 @@
 
 
 def per_tile(kernel, rows, weights, out_tail, tile):
+    weights = list(weights)
     count, dim = rows.shape
-    weight_bytes = sum(2 * w.size for w in weights)
+    specs = []
+    weight_bytes = 0
+    for k, w in enumerate(weights):
+        w, e = w if isinstance(w, tuple) else (w, None)
+        weights[k] = w
+        weight_bytes += 2 * w.shape[-2] * w.shape[-1]
+        specs.append(pl.BlockSpec(w.shape, lambda i: (0, 0)) if e is None else pl.BlockSpec((None,) + w.shape[1:], lambda i, e=e: (e, 0, 0)))
     out_size = count
     for n in out_tail:
         out_size *= n
     return pl.pallas_call(
         kernel,
         grid=(count // tile,),
-        in_specs=[pl.BlockSpec((tile, dim), lambda i: (i, 0))] + [pl.BlockSpec(w.shape, lambda i: (0, 0)) for w in weights],
+        in_specs=[pl.BlockSpec((tile, dim), lambda i: (i, 0))] + specs,
         out_specs=pl.BlockSpec((tile,) + out_tail, lambda i: (i,) + (0,) * len(out_tail)),
         out_shape=jax.ShapeDtypeStruct((count,) + out_tail, jnp.bfloat16),
         compiler_params=pltpu.CompilerParams(vmem_limit_bytes=56 * 2**20),
@@ -69,20 +76,25 @@
 
 
 def expert_hidden(rows, gate_w, up_w, tile):
-    return per_tile(hidden_kernel, rows, (gate_w, up_w), (gate_w.shape[1],), tile)
+    return per_tile(hidden_kernel, rows, (gate_w, up_w), (up_w.shape[1],), tile)
 
 
 def expert_down(hidden, downs, tile):
     return per_tile(down_kernel, hidden, downs, (sum(d.shape[1] for d in downs) // LANES, LANES), tile)
 
 
-def combine_kernel(per_group, top_k, part, pos_ref, gate_ref, *refs):
-    sources, (out_ref, held, sems) = refs[:-3], refs[-3:]
+def combine_kernel(per_group, top_k, part, pitch, pos_ref, gate_ref, *refs):
+    ins, (out_ref, held, sums, sems) = refs[:-4], refs[-4:]
+    sources = ins[:-1] if part else ins
     count, subs = sources[-1].shape[:2]
+    tokens_dev = out_ref.shape[0]
+    width = subs * LANES
     copies = []
     for k, src in enumerate(sources):
         src = src if src.shape[1] == subs else src.at[:, pl.ds(part * subs, subs), :]
         copies.append(pltpu.make_async_copy(src, held.at[pl.ds(k * count, count)], sems.at[k]))
+    if part:
+        copies.append(pltpu.make_async_copy(ins[-1], out_ref.at[:, pl.ds(0, width)], sems.at[len(sources)]))
     for copy in copies:
         copy.start()
     for copy in copies:
@@ -93,33 +105,48 @@
         for first in range(0, top_k, per_group):
             partial = None
             for j in range(first, first + per_group):
-                scaled = held[pos_ref[tok * top_k + j]].astype(jnp.float32) * gate_ref[tok * top_k + j]
+                gate = jnp.broadcast_to(gate_ref[tok, pl.ds(j, 1), :], (subs, LANES))
+                scaled = held[pos_ref[tok * top_k + j]].astype(jnp.float32) * gate
                 partial = scaled if partial is None else partial + scaled
             partial = partial.astype(jnp.bfloat16).astype(jnp.float32)
             total = partial if total is None else total + partial
-        out_ref[tok] = total.astype(jnp.bfloat16)
+        sums[pl.ds(tok, subs, stride=pitch), :] = total
         return carry
 
-    lax.fori_loop(0, out_ref.shape[0], one_token, 0, unroll=4)
-
-
-def combine(pos, gates, sources, part, per_group):
+    lax.fori_loop(0, tokens_dev, one_token, 0, unroll=8)
+
+    step = 128
+
+    def one_block(block, carry):
+        rows = pl.ds(pl.multiple_of(block * step, step), step)
+        for c in range(subs):
+            value = sums[pl.ds(pl.multiple_of(c * pitch + block * step, 8), step), :]
+            out_ref[rows, pl.ds(part * width + c * LANES, LANES)] = value.astype(jnp.bfloat16)
+        return carry
+
+    lax.fori_loop(0, tokens_dev // step, one_block, 0)
+
+
+def combine(pos, gates, sources, part, per_group, before):
     tokens_dev, top_k = pos.shape
     count, subs, _ = sources[-1].shape
-    smem = pl.BlockSpec(memory_space=pltpu.SMEM)
+    pitch = tokens_dev + 8
+    ins = list(sources) + list(before)
     hbm = pl.BlockSpec(memory_space=pl.ANY)
+    vmem = pl.BlockSpec(memory_space=pltpu.VMEM)
     return pl.pallas_call(
-        functools.partial(combine_kernel, per_group, top_k, part),
-        in_specs=[smem, smem] + [hbm] * len(sources),
-        out_specs=pl.BlockSpec(memory_space=pltpu.VMEM),
-        out_shape=jax.ShapeDtypeStruct((tokens_dev, subs, LANES), jnp.bfloat16),
+        functools.partial(combine_kernel, per_group, top_k, part, pitch),
+        in_specs=[pl.BlockSpec(memory_space=pltpu.SMEM), vmem] + [hbm] * len(ins),
+        out_specs=vmem,
+        out_shape=jax.ShapeDtypeStruct((tokens_dev, (part + 1) * subs * LANES), jnp.bfloat16),
         scratch_shapes=[
             pltpu.VMEM((count * len(sources), subs, LANES), jnp.bfloat16),
-            pltpu.SemaphoreType.DMA((len(sources),)),
+            pltpu.VMEM((subs * pitch, LANES), jnp.float32),
+            pltpu.SemaphoreType.DMA((len(ins),)),
         ],
-        compiler_params=pltpu.CompilerParams(vmem_limit_bytes=60 * 2**20),
+        compiler_params=pltpu.CompilerParams(vmem_limit_bytes=127 * 2**19),
         cost_estimate=pl.CostEstimate(flops=0, bytes_accessed=2 * count * subs * LANES * len(sources), transcendentals=0),
-    )(pos.reshape(-1), gates.reshape(-1), *sources)
+    )(pos.reshape(-1), gates, *ins)
 
 
 def solution(mesh):
@@ -143,26 +170,26 @@
         per_group, expert_cap = cap_sizes(tokens_dev, top_k, groups, group_exp)
         inner = lax.axis_index('ing')
 
-        first = w_gate[0]
-        first, rest_gate, rest_up, rest_down = lax.optimization_barrier((first, w_gate, w_up, w_down))
-        own = [(first if e == 0 else rest_gate[e], rest_up[e], rest_down[e]) for e in range(local_exp)]
+        own = [(w_up[e], w_down[e]) for e in range(local_exp)]
+        gate_left = lax.ppermute(w_gate, 'ing', ahead)
+        gate_right = lax.ppermute(w_gate, 'ing', behind)
         left = [tuple(lax.ppermute(w, 'ing', ahead) for w in own[e]) for e in range(local_exp)]
         right = [tuple(lax.ppermute(w, 'ing', behind) for w in own[e]) for e in range(local_exp)]
         far = []
         for e in range(local_exp):
-            gate_w = lax.ppermute(left[e][0], 'ing', ahead)
-            up_w = lax.ppermute(right[e][1], 'ing', behind)
+            gate_w = lax.ppermute(gate_left[e], 'ing', ahead)
+            up_w = lax.ppermute(right[e][0], 'ing', behind)
             pieces = 2 if e < local_exp - 1 else 4
             width = dim // pieces
             downs = []
             for q in range(pieces):
                 source, pairs = ((left, ahead), (right, behind))[q % 2]
-                downs.append(lax.ppermute(source[e][2][:, q * width:(q + 1) * width], 'ing', pairs))
+                downs.append(lax.ppermute(source[e][1][:, q * width:(q + 1) * width], 'ing', pairs))
             far.append((gate_w, up_w, tuple(downs)))
 
         shifts = (0, -1, 1, 2)
-        whole = lambda side: [(w[0], w[1], (w[2],)) for w in side]
-        held = {0: whole(own), -1: whole(left), 1: whole(right), 2: far}
+        whole = lambda gate, side: [((gate, e), up, (down,)) for e, (up, down) in enumerate(side)]
+        held = {0: whole(w_gate, own), -1: whole(gate_left, left), 1: whole(gate_right, right), 2: far}
         phases = [(0, e) for e in range(local_exp)]
         phases += [(s, e) for e in range(local_exp) for s in (-1, 1)]
         phases += [(2, e) for e in range(local_exp)]
@@ -218,10 +245,10 @@
                 backs.append(back.reshape(groups * expert_cap, subs, LANES))
             returned.append(backs)
         sources = [backs[0] for backs in returned[:-1]]
-        sides = []
+        gates = jnp.broadcast_to(gates[:, :, None], gates.shape + (LANES,))
+        out = []
         for part, back in enumerate(returned[-1]):
-            sides.append(combine(pos, gates, sources + [back], part, per_group))
-        return jnp.concatenate([side.reshape(tokens_dev, dim // 2) for side in sides], axis=1)
-
+            out = [combine(pos, gates, sources + [back], part, per_group, out)]
+        return out[0]
 
     return jax.shard_map(device_step, mesh=mesh, in_specs=(row_spec, row_spec, row_spec, weight_spec, weight_spec, weight_spec), out_specs=row_spec, check_vma=False)

time: 1270 us -> 1390 us (1.094)
  waiting for transfers between devices: 612 us -> 737 us
    ppermute x10 -> x12, waiting for transfers between devices: 92.4 us -> 192 us  [the longest x6 192 us: device_step(): lax.ppermute(source[e][1][:, q * width:(q + 1) * width], 'ing', pairs)]
    ppermute x6 -> x4, waiting for transfers between devices: 260 us -> 339 us  [device_step(): lax.ppermute(w, 'ing', ahead)]
    ppermute x6 -> x4, waiting for transfers between devices: 89.7 us -> 31.3 us  [device_step(): lax.ppermute(w, 'ing', behind)]
    all_to_all x9, waiting for transfers between devices: 97.9 us -> 61.7 us  [device_step(): lax.all_to_all(out.reshape(groups, expert_cap, subs, LANES), 'grp', 0, 0,...]
    ppermute x1, waiting for transfers between devices: 0.01 us -> 26.2 us  [device_step(): lax.ppermute(from_back[:mid], 'grp', chip_ahead)]
    gather x8, local copies, waits for them, and re-layouts: 168 us -> 187 us  [device_step(): rows = rows_all.at[index].get(mode='promise_in_bounds')]
    unnamed x61 -> x37, local copies, waits for them, and re-layouts: 48.5 us -> 36.7 us
  transfers between devices with their start and end apart: 41 -> 39, of which waited for: 18 -> 16; matrix products, arithmetic and copies ran while one was open for 20% -> 18% of each run, Pallas kernels for 19% -> 16%
where the time goes in v3:
time: 1390 us; the launch traced here: 1370 us
  waiting for transfers between devices  737 us (53%)
  Pallas kernels  269 us (19%)
  local copies, waits for them, and re-layouts  267 us (19%)
  starting transfers between devices  92 us (7%)
    ppermute x4, waiting for transfers between devices, device_step(): lax.ppermute(w, 'ing', ahead)  339 us
    pallas_call x10, Pallas kernels, per_tile(): pl.pallas_call(kernel, grid=(count // tile,), in_specs=[pl.BlockSpec((til...  223 us
    ppermute x6, waiting for transfers between devices, device_step(): lax.ppermute(source[e][1][:, q * width:(q + 1) * width], 'ing', pairs)  192 us
    gather x8, local copies, waits for them, and re-layouts, device_step(): rows = rows_all.at[index].get(mode='promise_in_bounds')  187 us
    ppermute x1, waiting for transfers between devices, device_step(): from_back = lax.ppermute(tokens, 'grp', chip_ahead)  81.2 us
    all_to_all x9, waiting for transfers between devices, device_step(): lax.all_to_all(out.reshape(groups, expert_cap, subs, LANES), 'grp', 0, 0,...  61.7 us
    all_to_all x9, starting transfers between devices, device_step(): lax.all_to_all(out.reshape(groups, expert_cap, subs, LANES), 'grp', 0, 0,...  49.2 us
    pallas_call x2, Pallas kernels, combine(): pl.pallas_call(functools.partial(combine_kernel, per_group, top_k, part,...  46.4 us
  transfers between devices with their start and end apart: 39, of which 16 were waited for; matrix products, arithmetic and copies ran while one was open for 18% of the time, Pallas kernels for 16%

profile of v3, /device:TPU:97, one launch (start us, length us, event | category | flops | bytes accessed | tf_op | source)
XLA Modules:
  0.0 1374.5 jit_solution(14613600025660083096)
XLA Ops:
  12.5 81.2 %collective-permute-done = bf16[1024,2048]{1,0:T(8,128)(2,1)} collective-permute-done((bf16[1024,2048]{1,0:T(8,128)(2,1)}, bf16[1024,2048]{1,0:T(8,128)(2,1)}, u32[]{:S(2)}, u32[]{:S(2)}) %collective-permute-start) | collective-permute-done | bytes 4194336 | tf_op jit(solution)/shard_map/ppermute | solution.py:199
  125.1 26.2 %collective-permute-done.2 = bf16[512,2048]{1,0:T(8,128)(2,1)S(1)} collective-permute-done((bf16[512,2048]{1,0:T(8,128)(2,1)}, bf16[512,2048]{1,0:T(8,128)(2,1)S(1)}, u32[]{:S(2)}, u32[]{:S(2)}) %collective-permute-start.2) | collective-permute-done | bytes 2097184 | tf_op jit(solution)/shard_map/ppermute | solution.py:201
  189.2 23.4 %gather_fusion = bf16[1536,2048]{1,0:T(8,128)(2,1)} fusion(bf16[8192,2048]{1,0:T(8,128)(2,1)} %constant_dynamic-update-slice_fusion, s32[2048]{0:T(1024)S(1)} %get-tuple-element.24), kind=kCustom, calls=%fused_computation | custom fusion | bytes 12589056 | tf_op jit(solution)/shard_map/gather | solution.py:232
  212.5 26.6 %shard_map.64 = bf16[1536,16,128]{2,1,0:T(8,128)(2,1)} custom-call(bf16[1536,2048]{1,0:T(8,128)(2,1)} %gather_fusion, bf16[2,2048,1024]{2,1,0:T(8,128)(2,1)} %gate_ref.3, bf16[2048,1024]{1,0:T(8,128)(2,1)} %get-tuple-element.18.up_ref, bf16[1024,2048]{1,0:T(8,128)(2,1)} %get-tuple-element.16.refs_0_), custom_call_target="tpu_custom_call" | custom-call | flops 19327352832 | bytes 25165824 | tf_op jit(solution)/shard_map/pallas_call | solution.py:63
  249.6 23.5 %gather_fusion.1 = bf16[1536,2048]{1,0:T(8,128)(2,1)} fusion(bf16[8192,2048]{1,0:T(8,128)(2,1)} %constant_dynamic-update-slice_fusion, s32[2048]{0:T(1024)S(1)} %get-tuple-element.23), kind=kCustom, calls=%fused_computation.1 | custom fusion | bytes 12589056 | tf_op jit(solution)/shard_map/gather | solution.py:232
  273.1 26.6 %shard_map.65 = bf16[1536,16,128]{2,1,0:T(8,128)(2,1)} custom-call(bf16[1536,2048]{1,0:T(8,128)(2,1)} %gather_fusion.1, bf16[2,2048,1024]{2,1,0:T(8,128)(2,1)} %gate_ref.3, bf16[2048,1024]{1,0:T(8,128)(2,1)} %get-tuple-element.17.up_ref, bf16[1024,2048]{1,0:T(8,128)(2,1)} %get-tuple-element.15.refs_0_), custom_call_target="tpu_custom_call" | custom-call | flops 19327352832 | bytes 25165824 | tf_op jit(solution)/shard_map/pallas_call | solution.py:63
  299.8 15.4 %all-to-all-done.1 = bf16[8,192,16,128]{3,2,1,0:T(8,128)(2,1)} async-done(((bf16[8,192,16,128]{3,2,1,0:T(8,128)(2,1)}), bf16[8,192,16,128]{3,2,1,0:T(8,128)(2,1)}, u32[]{:S(2)}, u32[]{:S(2)}) %all-to-all-start.1) | async-done | bytes 6291488 | tf_op jit(solution)/shard_map/all_to_all | solution.py:244
  325.4 23.3 %gather_fusion.2 = bf16[1536,2048]{1,0:T(8,128)(2,1)} fusion(bf16[8192,2048]{1,0:T(8,128)(2,1)} %constant_dynamic-update-slice_fusion, s32[2048]{0:T(1024)S(1)} %pad_clamp_fusion.5), kind=kCustom, calls=%fused_computation.2 | custom fusion | bytes 12589056 | tf_op jit(solution)/shard_map/gather | solution.py:232
  348.7 170.9 %collective-permute-done.10.up_ref = bf16[2048,1024]{1,0:T(8,128)(2,1)} collective-permute-done((bf16[2048,1024]{1,0:T(8,128)(2,1)}, bf16[2048,1024]{1,0:T(8,128)(2,1)}, u32[]{:S(2)}, u32[]{:S(2)}) %collective-permute-start.10) | collective-permute-done | bytes 4194336 | tf_op jit(solution)/shard_map/ppermute | solution.py:176
  521.0 88.1 %collective-permute-done.11.refs_0_ = bf16[1024,2048]{1,0:T(8,128)(2,1)} collective-permute-done((bf16[1024,2048]{1,0:T(8,128)(2,1)}, bf16[1024,2048]{1,0:T(8,128)(2,1)}, u32[]{:S(2)}, u32[]{:S(2)}) %collective-permute-start.11) | collective-permute-done | bytes 4194336 | tf_op jit(solution)/shard_map/ppermute | solution.py:176
  609.1 26.6 %shard_map.66 = bf16[1536,16,128]{2,1,0:T(8,128)(2,1)} custom-call(bf16[1536,2048]{1,0:T(8,128)(2,1)} %gather_fusion.2, bf16[2,2048,1024]{2,1,0:T(8,128)(2,1)} %collective-permute-done.9.gate_ref, bf16[2048,1024]{1,0:T(8,128)(2,1)} %collective-permute-done.10.up_ref, bf16[1024,2048]{1,0:T(8,128)(2,1)} %collective-permute-done.11.refs_0_), custom_call_target="tpu_custom_call" | custom-call | flops 19327352832 | bytes 25165824 | tf_op jit(solution)/shard_map/pallas_call | solution.py:63
  642.3 23.3 %gather_fusion.3 = bf16[1536,2048]{1,0:T(8,128)(2,1)} fusion(bf16[8192,2048]{1,0:T(8,128)(2,1)} %constant_dynamic-update-slice_fusion, s32[2048]{0:T(1024)S(1)} %pad_clamp_fusion.4), kind=kCustom, calls=%fused_computation.3 | custom fusion | bytes 12589056 | tf_op jit(solution)/shard_map/gather | solution.py:232
  665.6 18.9 %collective-permute-done.14.refs_0_ = bf16[1024,2048]{1,0:T(8,128)(2,1)} collective-permute-done((bf16[1024,2048]{1,0:T(8,128)(2,1)}, bf16[1024,2048]{1,0:T(8,128)(2,1)}, u32[]{:S(2)}, u32[]{:S(2)}) %collective-permute-start.14) | collective-permute-done | bytes 4194336 | tf_op jit(solution)/shard_map/ppermute | solution.py:177
  684.6 26.6 %shard_map.67 = bf16[1536,16,128]{2,1,0:T(8,128)(2,1)} custom-call(bf16[1536,2048]{1,0:T(8,128)(2,1)} %gather_fusion.3, bf16[2,2048,1024]{2,1,0:T(8,128)(2,1)} %collective-permute-done.12.gate_ref, bf16[2048,1024]{1,0:T(8,128)(2,1)} %collective-permute-done.13.up_ref, bf16[1024,2048]{1,0:T(8,128)(2,1)} %collective-permute-done.14.refs_0_), custom_call_target="tpu_custom_call" | custom-call | flops 19327352832 | bytes 25165824 | tf_op jit(solution)/shard_map/pallas_call | solution.py:63
  720.7 23.4 %gather_fusion.4 = bf16[1536,2048]{1,0:T(8,128)(2,1)} fusion(bf16[8192,2048]{1,0:T(8,128)(2,1)} %constant_dynamic-update-slice_fusion, s32[2048]{0:T(1024)S(1)} %pad_clamp_fusion.3), kind=kCustom, calls=%fused_computation.4 | custom fusion | bytes 12589056 | tf_op jit(solution)/shard_map/gather | solution.py:232
  744.1 80.2 %collective-permute-done.16.refs_0_ = bf16[1024,2048]{1,0:T(8,128)(2,1)} collective-permute-done((bf16[1024,2048]{1,0:T(8,128)(2,1)}, bf16[1024,2048]{1,0:T(8,128)(2,1)}, u32[]{:S(2)}, u32[]{:S(2)}) %collective-permute-start.16) | collective-permute-done | bytes 4194336 | tf_op jit(solution)/shard_map/ppermute | solution.py:176
  824.3 26.6 %shard_map.68 = bf16[1536,16,128]{2,1,0:T(8,128)(2,1)} custom-call(bf16[1536,2048]{1,0:T(8,128)(2,1)} %gather_fusion.4, bf16[2,2048,1024]{2,1,0:T(8,128)(2,1)} %collective-permute-done.9.gate_ref, bf16[2048,1024]{1,0:T(8,128)(2,1)} %collective-permute-done.15.up_ref, bf16[1024,2048]{1,0:T(8,128)(2,1)} %collective-permute-done.16.refs_0_), custom_call_target="tpu_custom_call" | custom-call | flops 19327352832 | bytes 25165824 | tf_op jit(solution)/shard_map/pallas_call | solution.py:63
  857.6 23.5 %gather_fusion.5 = bf16[1536,2048]{1,0:T(8,128)(2,1)} fusion(bf16[8192,2048]{1,0:T(8,128)(2,1)} %constant_dynamic-update-slice_fusion, s32[2048]{0:T(1024)S(1)} %pad_clamp_fusion.2), kind=kCustom, calls=%fused_computation.5 | custom fusion | bytes 12589056 | tf_op jit(solution)/shard_map/gather | solution.py:232
  888.0 12.4 collective-permute-done.18.refs_0_
  900.3 26.6 %shard_map.69 = bf16[1536,16,128]{2,1,0:T(8,128)(2,1)} custom-call(bf16[1536,2048]{1,0:T(8,128)(2,1)} %gather_fusion.5, bf16[2,2048,1024]{2,1,0:T(8,128)(2,1)} %collective-permute-done.12.gate_ref, bf16[2048,1024]{1,0:T(8,128)(2,1)} %collective-permute-done.17.up_ref, bf16[1024,2048]{1,0:T(8,128)(2,1)} %collective-permute-done.18.refs_0_), custom_call_target="tpu_custom_call" | custom-call | flops 19327352832 | bytes 25165824 | tf_op jit(solution)/shard_map/pallas_call | solution.py:63
  948.9 23.4 %gather_fusion.7 = bf16[1536,2048]{1,0:T(8,128)(2,1)} fusion(bf16[8192,2048]{1,0:T(8,128)(2,1)} %constant_dynamic-update-slice_fusion, s32[2048]{0:T(1024)S(1)} %pad_clamp_fusion), kind=kCustom, calls=%fused_computation.7 | custom fusion | bytes 12589056 | tf_op jit(solution)/shard_map/gather | solution.py:232
  972.3 120.1 %collective-permute-done.27.refs_0_ = bf16[1024,512]{1,0:T(8,128)(2,1)S(1)} collective-permute-done((bf16[1024,512]{1,0:T(8,128)(2,1)S(1)}, bf16[1024,512]{1,0:T(8,128)(2,1)S(1)}, u32[]{:S(2)}, u32[]{:S(2)}) %collective-permute-start.27) | collective-permute-done | bytes 1048608 | tf_op jit(solution)/shard_map/ppermute | solution.py:187
  1095.4 18.7 %shard_map.71.x_ref = bf16[1536,1024]{1,0:T(8,128)(2,1)} custom-call(bf16[1536,2048]{1,0:T(8,128)(2,1)} %gather_fusion.7, bf16[2048,1024]{1,0:T(8,128)(2,1)} %collective-permute-done.23.gate_ref, bf16[2048,1024]{1,0:T(8,128)(2,1)} %collective-permute-done.24.up_ref), custom_call_target="tpu_custom_call" | custom-call | flops 12884901888 | bytes 17825792 | tf_op jit(solution)/shard_map/pallas_call | solution.py:63
  1114.1 48.4 %collective-permute-done.28.refs_1_ = bf16[1024,512]{1,0:T(8,128)(2,1)S(1)} collective-permute-done((bf16[1024,512]{1,0:T(8,128)(2,1)S(1)}, bf16[1024,512]{1,0:T(8,128)(2,1)S(1)}, u32[]{:S(2)}, u32[]{:S(2)}) %collective-permute-start.28) | collective-permute-done | bytes 1048608 | tf_op jit(solution)/shard_map/ppermute | solution.py:187
  1163.5 8.4 shard_map.73
  1178.3 23.3 %gather_fusion.6 = bf16[1536,2048]{1,0:T(8,128)(2,1)} fusion(bf16[8192,2048]{1,0:T(8,128)(2,1)} %constant_dynamic-update-slice_fusion, s32[2048]{0:T(1024)S(1)} %pad_clamp_fusion.1), kind=kCustom, calls=%fused_computation.6 | custom fusion | bytes 12589056 | tf_op jit(solution)/shard_map/gather | solution.py:232
  1201.6 27.5 %shard_map.70 = bf16[1536,16,128]{2,1,0:T(8,128)(2,1)} custom-call(bf16[1536,2048]{1,0:T(8,128)(2,1)} %gather_fusion.6, bf16[2048,1024]{1,0:T(8,128)(2,1)} %collective-permute-done.19.gate_ref, bf16[2048,1024]{1,0:T(8,128)(2,1)} %collective-permute-done.20.up_ref, bf16[1024,1024]{1,0:T(8,128)(2,1)} %collective-permute-done.21.refs_0_, ...), custom_call_target="tpu_custom_call" | custom-call | flops 19327352832 | bytes 25165824 | tf_op jit(solution)/shard_map/pallas_call | solution.py:63
  1239.3 23.6 %collective-permute-done.25.refs_0_ = bf16[1024,512]{1,0:T(8,128)(2,1)S(1)} collective-permute-done((bf16[1024,512]{1,0:T(8,128)(2,1)}, bf16[1024,512]{1,0:T(8,128)(2,1)S(1)}, u32[]{:S(2)}, u32[]{:S(2)}) %collective-permute-start.25) | collective-permute-done | bytes 1048608 | tf_op jit(solution)/shard_map/ppermute | solution.py:187
  1273.3 34.0 %all-to-all-done.7 = bf16[8,192,16,128]{3,2,1,0:T(8,128)(2,1)} async-done(((bf16[8,192,16,128]{3,2,1,0:T(8,128)(2,1)}), bf16[8,192,16,128]{3,2,1,0:T(8,128)(2,1)}, u32[]{:S(2)}, u32[]{:S(2)}) %all-to-all-start.7) | async-done | bytes 6291488 | tf_op jit(solution)/shard_map/all_to_all | solution.py:244
  1317.4 22.6 %shard_map.74.refs_8_ = bf16[1024,1024]{1,0:T(8,128)(2,1)} custom-call(s32[8192]{0:T(1024)} %fusion.11.pos_ref, f32[1024,8,128]{2,1,0:T(8,128)} %broadcast_in_dim.111.gate_ref, bf16[1536,16,128]{2,1,0:T(8,128)(2,1)} %bitcast.4.refs_0_, bf16[1536,16,128]{2,1,0:T(8,128)(2,1)} %bitcast.8.refs_1_, bf16[1536,16,128]{2,1,0:T(8,128)(2,1)} %bitcast.10.refs_2_, ...), custom_call_target="tpu_custom_call" | custom-call | bytes 25165824 | tf_op jit(solution)/shard_map/pallas_call | solution.py:137
  1340.0 10.2 all-to-all-done.8
  1350.1 23.8 %shard_map.75 = bf16[1024,2048]{1,0:T(8,128)(2,1)} custom-call(s32[8192]{0:T(1024)} %fusion.11.pos_ref, f32[1024,8,128]{2,1,0:T(8,128)} %broadcast_in_dim.111.gate_ref, bf16[1536,16,128]{2,1,0:T(8,128)(2,1)} %bitcast.4.refs_0_, bf16[1536,16,128]{2,1,0:T(8,128)(2,1)} %bitcast.8.refs_1_, bf16[1536,16,128]{2,1,0:T(8,128)(2,1)} %bitcast.10.refs_2_, ...), custom_call_target="tpu_custom_call" | custom-call | bytes 25165824 | tf_op jit(solution)/shard_map/pallas_call | solution.py:137
  (158 shorter events, 196.1 us)
Async XLA Ops:
  0.0 93.7 %collective-permute-start = (bf16[1024,2048]{1,0:T(8,128)(2,1)}, bf16[1024,2048]{1,0:T(8,128)(2,1)}, u32[]{:S(2)}, u32[]{:S(2)}) collective-permute-start(bf16[1024,2048]{1,0:T(8,128)(2,1)} %param.6), channel_id=1, source_target_pairs={{0,2},{1,3},{2,4},{3,5},{4,6},{5,7},{6,0},{7,1},{8,10},{9,11},{10,... | collective-permute-start | bytes 12582920 | tf_op jit(solution)/shard_map/ppermute | solution.py:199
  2.2 102.0 %collective-permute-start.1 = (bf16[1024,2048]{1,0:T(8,128)(2,1)}, bf16[1024,2048]{1,0:T(8,128)(2,1)}, u32[]{:S(2)}, u32[]{:S(2)}) collective-permute-start(bf16[1024,2048]{1,0:T(8,128)(2,1)} %param.6), channel_id=1, source_target_pairs={{0,6},{1,7},{2,0},{3,1},{4,2},{5,3},{6,4},{7,5},{8,14},{9,15},{10,... | collective-permute-start | bytes 12582920 | tf_op jit(solution)/shard_map/ppermute | solution.py:200
  3.7 168.3 %collective-permute-start.4 = (bf16[1024,2048]{1,0:T(8,128)(2,1)}, bf16[1024,2048]{1,0:T(8,128)(2,1)}, u32[]{:S(2)}, u32[]{:S(2)}) collective-permute-start(bf16[1024,2048]{1,0:T(8,128)(2,1)} %param.6), channel_id=1, source_target_pairs={{0,1},{1,0},{2,3},{3,2},{4,5},{5,4},{6,7},{7,6},{8,9},{9,8},{10,11... | collective-permute-start | bytes 12582920 | tf_op jit(solution)/shard_map/ppermute | solution.py:203
  93.7 83.0 %collective-permute-start.5 = (bf16[1024,2048]{1,0:T(8,128)(2,1)}, bf16[1024,2048]{1,0:T(8,128)(2,1)}, u32[]{:S(2)}, u32[]{:S(2)}) collective-permute-start(bf16[1024,2048]{1,0:T(8,128)(2,1)} %collective-permute-done), channel_id=1, source_target_pairs={{0,1},{1,0},{2,3},{3,2},{4,5},{5,4},{6,7},{7,6},{8,9},{9,8},{10,11... | collective-permute-start | bytes 12582920 | tf_op jit(solution)/shard_map/ppermute | solution.py:203
  102.9 48.5 %collective-permute-start.2 = (bf16[512,2048]{1,0:T(8,128)(2,1)}, bf16[512,2048]{1,0:T(8,128)(2,1)S(1)}, u32[]{:S(2)}, u32[]{:S(2)}) collective-permute-start(bf16[512,2048]{1,0:T(8,128)(2,1)} %slice.72), channel_id=1, source_target_pairs={{0,2},{1,3},{2,4},{3,5},{4,6},{5,7},{6,0},{7,1},{8,10},{9,11},{10,... | collective-permute-start | bytes 6291464 | tf_op jit(solution)/shard_map/ppermute | solution.py:201
  104.1 77.3 %collective-permute-start.6 = (bf16[1024,2048]{1,0:T(8,128)(2,1)}, bf16[1024,2048]{1,0:T(8,128)(2,1)}, u32[]{:S(2)}, u32[]{:S(2)}) collective-permute-start(bf16[1024,2048]{1,0:T(8,128)(2,1)} %collective-permute-done.1), channel_id=1, source_target_pairs={{0,1},{1,0},{2,3},{3,2},{4,5},{5,4},{6,7},{7,6},{8,9},{9,8},{10,11... | collective-permute-start | bytes 12582920 | tf_op jit(solution)/shard_map/ppermute | solution.py:203
  239.1 76.0 %all-to-all-start.1 = ((bf16[8,192,16,128]{3,2,1,0:T(8,128)(2,1)}), bf16[8,192,16,128]{3,2,1,0:T(8,128)(2,1)}, u32[]{:S(2)}, u32[]{:S(2)}) async-start(bf16[8,192,16,128]{3,2,1,0:T(8,128)(2,1)} %bitcast.39), calls=%async_computation.1 | async-start | bytes 12582912 | tf_op jit(solution)/shard_map/all_to_all | solution.py:244
  243.9 365.1 %collective-permute-start.9 = (bf16[2,2048,1024]{2,1,0:T(8,128)(2,1)}, bf16[2,2048,1024]{2,1,0:T(8,128)(2,1)}, u32[]{:S(2)}, u32[]{:S(2)}) collective-permute-start(bf16[2,2048,1024]{2,1,0:T(8,128)(2,1)} %gate_ref.3), channel_id=1, source_target_pairs={{0,8},{8,16},{16,24},{24,0},{1,9},{9,17},{17,25},{25,1},{2,10},{10... | collective-permute-start | bytes 25165832 | tf_op jit(solution)/shard_map/ppermute | solution.py:174
  245.9 273.7 %collective-permute-start.10 = (bf16[2048,1024]{1,0:T(8,128)(2,1)}, bf16[2048,1024]{1,0:T(8,128)(2,1)}, u32[]{:S(2)}, u32[]{:S(2)}) collective-permute-start(bf16[2048,1024]{1,0:T(8,128)(2,1)} %get-tuple-element.18.up_ref), channel_id=1, source_target_pairs={{0,8},{8,16},{16,24},{24,0},{1,9},{9,17},{17,25},{25,1},{2,10},{10... | collective-permute-start | bytes 12582920 | tf_op jit(solution)/shard_map/ppermute | solution.py:176
  247.8 361.3 %collective-permute-start.11 = (bf16[1024,2048]{1,0:T(8,128)(2,1)}, bf16[1024,2048]{1,0:T(8,128)(2,1)}, u32[]{:S(2)}, u32[]{:S(2)}) collective-permute-start(bf16[1024,2048]{1,0:T(8,128)(2,1)} %get-tuple-element.16.refs_0_), channel_id=1, source_target_pairs={{0,8},{8,16},{16,24},{24,0},{1,9},{9,17},{17,25},{25,1},{2,10},{10... | collective-permute-start | bytes 12582920 | tf_op jit(solution)/shard_map/ppermute | solution.py:176
  315.1 320.6 %all-to-all-start.2 = ((bf16[8,192,16,128]{3,2,1,0:T(8,128)(2,1)}), bf16[8,192,16,128]{3,2,1,0:T(8,128)(2,1)}, u32[]{:S(2)}, u32[]{:S(2)}) async-start(bf16[8,192,16,128]{3,2,1,0:T(8,128)(2,1)} %bitcast.34), calls=%async_computation.2 | async-start | bytes 12582912 | tf_op jit(solution)/shard_map/all_to_all | solution.py:244
  320.6 363.9 %collective-permute-start.12 = (bf16[2,2048,1024]{2,1,0:T(8,128)(2,1)}, bf16[2,2048,1024]{2,1,0:T(8,128)(2,1)}, u32[]{:S(2)}, u32[]{:S(2)}) collective-permute-start(bf16[2,2048,1024]{2,1,0:T(8,128)(2,1)} %gate_ref.3), channel_id=1, source_target_pairs={{0,24},{8,0},{16,8},{24,16},{1,25},{9,1},{17,9},{25,17},{2,26},{10... | collective-permute-start | bytes 25165832 | tf_op jit(solution)/shard_map/ppermute | solution.py:175
  325.1 340.6 %collective-permute-start.13 = (bf16[2048,1024]{1,0:T(8,128)(2,1)}, bf16[2048,1024]{1,0:T(8,128)(2,1)}, u32[]{:S(2)}, u32[]{:S(2)}) collective-permute-start(bf16[2048,1024]{1,0:T(8,128)(2,1)} %get-tuple-element.18.up_ref), channel_id=1, source_target_pairs={{0,24},{8,0},{16,8},{24,16},{1,25},{9,1},{17,9},{25,17},{2,26},{10... | collective-permute-start | bytes 12582920 | tf_op jit(solution)/shard_map/ppermute | solution.py:177
  519.6 165.0 %collective-permute-start.14 = (bf16[1024,2048]{1,0:T(8,128)(2,1)}, bf16[1024,2048]{1,0:T(8,128)(2,1)}, u32[]{:S(2)}, u32[]{:S(2)}) collective-permute-start(bf16[1024,2048]{1,0:T(8,128)(2,1)} %get-tuple-element.16.refs_0_), channel_id=1, source_target_pairs={{0,24},{8,0},{16,8},{24,16},{1,25},{9,1},{17,9},{25,17},{2,26},{10... | collective-permute-start | bytes 12582920 | tf_op jit(solution)/shard_map/ppermute | solution.py:177
  635.7 76.5 %all-to-all-start.3 = ((bf16[8,192,16,128]{3,2,1,0:T(8,128)(2,1)}), bf16[8,192,16,128]{3,2,1,0:T(8,128)(2,1)}, u32[]{:S(2)}, u32[]{:S(2)}) async-start(bf16[8,192,16,128]{3,2,1,0:T(8,128)(2,1)} %bitcast.36), calls=%async_computation.3 | async-start | bytes 12582912 | tf_op jit(solution)/shard_map/all_to_all | solution.py:244
  640.9 103.2 %collective-permute-start.15 = (bf16[2048,1024]{1,0:T(8,128)(2,1)}, bf16[2048,1024]{1,0:T(8,128)(2,1)}, u32[]{:S(2)}, u32[]{:S(2)}) collective-permute-start(bf16[2048,1024]{1,0:T(8,128)(2,1)} %get-tuple-element.17.up_ref), channel_id=1, source_target_pairs={{0,8},{8,16},{16,24},{24,0},{1,9},{9,17},{17,25},{25,1},{2,10},{10... | collective-permute-start | bytes 12582920 | tf_op jit(solution)/shard_map/ppermute | solution.py:176
  640.9 183.3 %collective-permute-start.16 = (bf16[1024,2048]{1,0:T(8,128)(2,1)}, bf16[1024,2048]{1,0:T(8,128)(2,1)}, u32[]{:S(2)}, u32[]{:S(2)}) collective-permute-start(bf16[1024,2048]{1,0:T(8,128)(2,1)} %get-tuple-element.15.refs_0_), channel_id=1, source_target_pairs={{0,8},{8,16},{16,24},{24,0},{1,9},{9,17},{17,25},{25,1},{2,10},{10... | collective-permute-start | bytes 12582920 | tf_op jit(solution)/shard_map/ppermute | solution.py:176
  712.2 138.7 %all-to-all-start.4 = ((bf16[8,192,16,128]{3,2,1,0:T(8,128)(2,1)}), bf16[8,192,16,128]{3,2,1,0:T(8,128)(2,1)}, u32[]{:S(2)}, u32[]{:S(2)}) async-start(bf16[8,192,16,128]{3,2,1,0:T(8,128)(2,1)} %bitcast.38), calls=%async_computation.4 | async-start | bytes 12582912 | tf_op jit(solution)/shard_map/all_to_all | solution.py:244
  717.9 138.9 %collective-permute-start.17 = (bf16[2048,1024]{1,0:T(8,128)(2,1)}, bf16[2048,1024]{1,0:T(8,128)(2,1)}, u32[]{:S(2)}, u32[]{:S(2)}) collective-permute-start(bf16[2048,1024]{1,0:T(8,128)(2,1)} %get-tuple-element.17.up_ref), channel_id=1, source_target_pairs={{0,24},{8,0},{16,8},{24,16},{1,25},{9,1},{17,9},{25,17},{2,26},{10... | collective-permute-start | bytes 12582920 | tf_op jit(solution)/shard_map/ppermute | solution.py:177
  720.6 179.7 %collective-permute-start.18 = (bf16[1024,2048]{1,0:T(8,128)(2,1)}, bf16[1024,2048]{1,0:T(8,128)(2,1)}, u32[]{:S(2)}, u32[]{:S(2)}) collective-permute-start(bf16[1024,2048]{1,0:T(8,128)(2,1)} %get-tuple-element.15.refs_0_), channel_id=1, source_target_pairs={{0,24},{8,0},{16,8},{24,16},{1,25},{9,1},{17,9},{25,17},{2,26},{10... | collective-permute-start | bytes 12582920 | tf_op jit(solution)/shard_map/ppermute | solution.py:177
  850.9 77.2 %all-to-all-start.5 = ((bf16[8,192,16,128]{3,2,1,0:T(8,128)(2,1)}), bf16[8,192,16,128]{3,2,1,0:T(8,128)(2,1)}, u32[]{:S(2)}, u32[]{:S(2)}) async-start(bf16[8,192,16,128]{3,2,1,0:T(8,128)(2,1)} %bitcast.35), calls=%async_computation.5 | async-start | bytes 12582912 | tf_op jit(solution)/shard_map/all_to_all | solution.py:244
  856.9 235.5 %collective-permute-start.24 = (bf16[2048,1024]{1,0:T(8,128)(2,1)}, bf16[2048,1024]{1,0:T(8,128)(2,1)}, u32[]{:S(2)}, u32[]{:S(2)}) collective-permute-start(bf16[2048,1024]{1,0:T(8,128)(2,1)} %collective-permute-done.17.up_ref), channel_id=1, source_target_pairs={{0,24},{8,0},{16,8},{24,16},{1,25},{9,1},{17,9},{25,17},{2,26},{10... | collective-permute-start | bytes 12582920 | tf_op jit(solution)/shard_map/ppermute | solution.py:181
  887.1 208.0 %collective-permute-start.23 = (bf16[2048,1024]{1,0:T(8,128)(2,1)}, bf16[2048,1024]{1,0:T(8,128)(2,1)}, u32[]{:S(2)}, u32[]{:S(2)}) collective-permute-start(bf16[2048,1024]{1,0:T(8,128)(2,1)} %get-tuple-element.13), channel_id=1, source_target_pairs={{0,8},{8,16},{16,24},{24,0},{1,9},{9,17},{17,25},{25,1},{2,10},{10... | collective-permute-start | bytes 12582920 | tf_op jit(solution)/shard_map/ppermute | solution.py:180
  928.1 243.9 %all-to-all-start.6 = ((bf16[8,192,16,128]{3,2,1,0:T(8,128)(2,1)}), bf16[8,192,16,128]{3,2,1,0:T(8,128)(2,1)}, u32[]{:S(2)}, u32[]{:S(2)}) async-start(bf16[8,192,16,128]{3,2,1,0:T(8,128)(2,1)} %bitcast.33), calls=%async_computation.6 | async-start | bytes 12582912 | tf_op jit(solution)/shard_map/all_to_all | solution.py:244
  933.8 267.8 %collective-permute-start.20 = (bf16[2048,1024]{1,0:T(8,128)(2,1)}, bf16[2048,1024]{1,0:T(8,128)(2,1)}, u32[]{:S(2)}, u32[]{:S(2)}) collective-permute-start(bf16[2048,1024]{1,0:T(8,128)(2,1)} %collective-permute-done.13.up_ref), channel_id=1, source_target_pairs={{0,24},{8,0},{16,8},{24,16},{1,25},{9,1},{17,9},{25,17},{2,26},{10... | collective-permute-start | bytes 12582920 | tf_op jit(solution)/shard_map/ppermute | solution.py:181
  937.2 264.4 %collective-permute-start.19 = (bf16[2048,1024]{1,0:T(8,128)(2,1)}, bf16[2048,1024]{1,0:T(8,128)(2,1)}, u32[]{:S(2)}, u32[]{:S(2)}) collective-permute-start(bf16[2048,1024]{1,0:T(8,128)(2,1)} %get-tuple-element.14), channel_id=1, source_target_pairs={{0,8},{8,16},{16,24},{24,0},{1,9},{9,17},{17,25},{25,1},{2,10},{10... | collective-permute-start | bytes 12582920 | tf_op jit(solution)/shard_map/ppermute | solution.py:180
  939.9 152.5 %collective-permute-start.27 = (bf16[1024,512]{1,0:T(8,128)(2,1)S(1)}, bf16[1024,512]{1,0:T(8,128)(2,1)S(1)}, u32[]{:S(2)}, u32[]{:S(2)}) collective-permute-start(bf16[1024,512]{1,0:T(8,128)(2,1)S(1)} %get-tuple-element.21), channel_id=1, source_target_pairs={{0,8},{8,16},{16,24},{24,0},{1,9},{9,17},{17,25},{25,1},{2,10},{10... | collective-permute-start | bytes 3145736 | tf_op jit(solution)/shard_map/ppermute | solution.py:187
  1092.4 109.2 %collective-permute-start.21 = (bf16[1024,1024]{1,0:T(8,128)(2,1)}, bf16[1024,1024]{1,0:T(8,128)(2,1)}, u32[]{:S(2)}, u32[]{:S(2)}) collective-permute-start(bf16[1024,1024]{1,0:T(8,128)(2,1)} %slice.75), channel_id=1, source_target_pairs={{0,8},{8,16},{16,24},{24,0},{1,9},{9,17},{17,25},{25,1},{2,10},{10... | collective-permute-start | bytes 6291464 | tf_op jit(solution)/shard_map/ppermute | solution.py:187
  1092.4 109.2 %collective-permute-start.22 = (bf16[1024,1024]{1,0:T(8,128)(2,1)}, bf16[1024,1024]{1,0:T(8,128)(2,1)}, u32[]{:S(2)}, u32[]{:S(2)}) collective-permute-start(bf16[1024,1024]{1,0:T(8,128)(2,1)} %slice.76), channel_id=1, source_target_pairs={{0,24},{8,0},{16,8},{24,16},{1,25},{9,1},{17,9},{25,17},{2,26},{10... | collective-permute-start | bytes 6291464 | tf_op jit(solution)/shard_map/ppermute | solution.py:187
  1095.1 67.5 %collective-permute-start.28 = (bf16[1024,512]{1,0:T(8,128)(2,1)S(1)}, bf16[1024,512]{1,0:T(8,128)(2,1)S(1)}, u32[]{:S(2)}, u32[]{:S(2)}) collective-permute-start(bf16[1024,512]{1,0:T(8,128)(2,1)S(1)} %get-tuple-element.19), channel_id=1, source_target_pairs={{0,24},{8,0},{16,8},{24,16},{1,25},{9,1},{17,9},{25,17},{2,26},{10... | collective-permute-start | bytes 3145736 | tf_op jit(solution)/shard_map/ppermute | solution.py:187
  1172.0 57.2 %all-to-all-start.9 = ((bf16[8,192,8,128]{3,2,1,0:T(8,128)(2,1)}), bf16[8,192,8,128]{3,2,1,0:T(8,128)(2,1)S(1)}, u32[]{:S(2)}, u32[]{:S(2)}) async-start(bf16[8,192,8,128]{3,2,1,0:T(8,128)(2,1)} %bitcast.41), calls=%async_computation.9 | async-start | bytes 6291456 | tf_op jit(solution)/shard_map/all_to_all | solution.py:244
  1230.8 76.5 %all-to-all-start.7 = ((bf16[8,192,16,128]{3,2,1,0:T(8,128)(2,1)}), bf16[8,192,16,128]{3,2,1,0:T(8,128)(2,1)}, u32[]{:S(2)}, u32[]{:S(2)}) async-start(bf16[8,192,16,128]{3,2,1,0:T(8,128)(2,1)} %bitcast.37), calls=%async_computation.7 | async-start | bytes 12582912 | tf_op jit(solution)/shard_map/all_to_all | solution.py:244
  (21 other events, 585.3 us)
